TPU v7x, 512 devices: a whole 4x8x8 slice. The times are simulated.
512 devices in a mesh: gx: 8 (over z), gy: 8 (over y), gz: 8 (over x, core).
Axes of the slice: x: 4, y: 8, z: 8, core: 2. Of those that a mesh axis runs over, the one named last changes fastest.
Arguments:
- ref_pos: float32 [4096, 3, 128], P(('gx', 'gy', 'gz')), may hold values from -0.1 to 512, as said below
- displace: float32 [4096, 3, 128], P(('gx', 'gy', 'gz')), may hold values from -0.1 to 0.1
- velocity: float32 [4096, 3, 128], P(('gx', 'gy', 'gz')), may hold values from -15 to 15
- acceleration: float32 [4096, 3, 128], P(('gx', 'gy', 'gz')), may hold values from -6 to 6
- new_owner: int32 [4096], P(('gx', 'gy', 'gz')), may hold values from 0 to 511, as said below
- ghost_ids: int32 [12288], P(('gx', 'gy', 'gz')), may hold values from 0 to 4095, as said below
- pair_blocks: int32 [2, 110592], P(None, ('gx', 'gy', 'gz')), may hold values from 0 to 31, as said below
- pair_count: int32 [512], P(('gx', 'gy', 'gz')), may hold values from 1 to 216, as said below
- bond_bits: int32 [110592, 12, 128], P(('gx', 'gy', 'gz')), may hold values from 0 to 2047, as said below
Outputs:
- displace_new: float32 [4096, 3, 128], P(('gx', 'gy', 'gz'))
- velocity_new: float32 [4096, 3, 128], P(('gx', 'gy', 'gz'))
- acceleration_new: float32 [4096, 3, 128], P(('gx', 'gy', 'gz'))
Inputs may be any that keep to these rules, and one draw needn't show every extreme that they name: `new_owner`: each block's new owner is its own device or one of the 26 devices around it in the grid gx by gy by gz, wrapping around every axis; exactly 2 blocks of each device get another owner, and every device is the new owner of exactly 8 blocks. `ghost_ids`: block indices in the new layout; each names a block whose new owner is one of the 26 devices around the device of the list, wrapping around; a list may name a block more than once; a list names at most 3 entries whose blocks have the same owner, and exactly 3 for some owner in every list. `pair_blocks`: row 0 is a slot of the device (below 8); row 1 is an index into the device's 8 blocks followed by its 24 ghost blocks. `pair_count`: at least one device has all 216 slots live in every draw. `bond_bits`: bits of particles at 128 or beyond are not used. `ref_pos`: reference positions of two different particles are at least 0.65 apart.
All inputs are finite; a program needn't handle non-finite values. Where the computation divides by a largest or mean magnitude, that divisor is 1e-20 or more.
Results may differ from a plain program's by a relative error of at most 0.0003.
Values sent between devices are 32-bit elements; how exact they have to be, the bound alone decides.
No kernel may reach another device: no remote copies, remote signals or barrier semaphores. Data moves between devices by JAX's collectives and lax.ppermute only.
A program may use at most 64 MiB of HBM per device.

v0:
```python
import jax
import jax.numpy as jnp
import numpy as np
from jax import lax
from jax.experimental import pallas as pl
from jax.experimental.pallas import tpu as pltpu
from jax.sharding import Mesh
from jax.sharding import PartitionSpec as P

WORD_BITS = 11
GX = ("gx_half", "gx_odd")
GY = ("gy_half", "gy_odd")
GZ = ("gz_half", "gz_odd")
AXES = (GX, GY, GZ)
ALL = GX + GY + GZ
LATTICE = ("gx_half", "gy_half", "gz_half")

courant = 0.05
stiffness = 20.0


COMPS = 12
PACK = 32
CELL = 104
GROUP = 8
STEADY = 3


LANE_GATHER = lax.GatherDimensionNumbers(
    offset_dims=(),
    collapsed_slice_dims=(1,),
    start_index_map=(1,),
    operand_batching_dims=(0,),
    start_indices_batching_dims=(0,),
)


def by_lane(table, particle):
    return lax.gather(
        table,
        particle[:, :, None],
        LANE_GATHER,
        slice_sizes=(1, 1),
        mode=lax.GatherScatterMode.PROMISE_IN_BOUNDS,
    )


def prepare_kernel(words_ref, wide_ref, most_ref):
    pairs = words_ref.shape[1]

    def group(g, carry):
        start = pl.multiple_of(g * GROUP, GROUP)
        words = [words_ref[w, pl.ds(start, GROUP), :] for w in range(12)]
        most = None
        for t in range(4):
            total = None
            for w in range(12):
                move = WORD_BITS * w - 32 * t
                if -WORD_BITS < move < 32:
                    part = words[w] << move if move >= 0 else words[w] >> -move
                    total = part if total is None else total | part
            wide_ref[t, pl.ds(start, GROUP), :] = total
            wide_ref[4 + t, pl.ds(start, GROUP), :] = total
            used = lax.population_count(total)
            most = used if most is None else jnp.maximum(most, used)
        most_ref[pl.ds(g, 1), :] = jnp.full((1, 128), jnp.max(most), jnp.int32)
        return carry

    lax.fori_loop(0, pairs // GROUP, group, 0)


def call_prepare(bond_bits):
    pairs = bond_bits.shape[0]
    vmem = pl.BlockSpec(memory_space=pltpu.VMEM)
    wide, most = pl.pallas_call(
        prepare_kernel,
        out_shape=(
            jax.ShapeDtypeStruct((8, pairs, 128), jnp.int32),
            jax.ShapeDtypeStruct((pairs // GROUP, 128), jnp.int32),
        ),
        in_specs=[vmem],
        out_specs=(vmem, vmem),
        cost_estimate=pl.CostEstimate(
            flops=20_000_000, bytes_accessed=2_200_000, transcendentals=0
        ),
        name="prepare",
    )(jnp.transpose(bond_bits, (1, 0, 2)))
    return wide.reshape(8 * pairs, 128), most


def self_bits():
    bit = np.arange(128)[None, :] - 32 * (np.arange(8)[:, None] % 4)
    lost = np.where((bit >= 0) & (bit < 32), np.int64(1) << np.clip(bit, 0, 31), 0)
    return (~lost).astype(np.uint32).view(np.int32)


def pack_kernel(owner_ref, self_ref, ref_ref, dis_ref, vel_ref, acc_ref, out_ref, top_ref):
    myself = self_ref[0]
    first = jnp.int32(0)
    second = jnp.int32(0)
    found = jnp.bool_(False)
    for k in range(8):
        leaves = owner_ref[k] != myself
        first = jnp.where(leaves & jnp.logical_not(found), k, first)
        second = jnp.where(leaves & found, k, second)
        found = found | leaves
    for group, source in enumerate((ref_ref, dis_ref, vel_ref, acc_ref)):
        for c in range(3):
            out_ref[pl.ds(group * 3 + c, 1), :] = source[c, pl.ds(first, 1), :]
            out_ref[pl.ds(12 + group * 3 + c, 1), :] = source[c, pl.ds(second, 1), :]
    lane = lax.broadcasted_iota(jnp.int32, (8, 128), 1)
    values = (
        owner_ref[first],
        owner_ref[second],
        myself * 8 + first,
        myself * 8 + second,
    )
    misc = jnp.zeros((8, 128), jnp.float32)
    for place, value in enumerate(values):
        misc = jnp.where(lane == place, value.astype(jnp.float32), misc)
    speed = jnp.maximum(
        jnp.maximum(jnp.abs(vel_ref[0]), jnp.abs(vel_ref[1])), jnp.abs(vel_ref[2])
    )
    out_ref[24:32, :] = misc
    top_ref[...] = jnp.full(top_ref.shape, jnp.max(speed), jnp.float32)


def settle_kernel(
    owner_ref, self_ref, ref_ref, dis_ref, vel_ref, acc_ref, cand_ref, tops_ref, out_ref
):
    myself = self_ref[0]
    misc = cand_ref[pl.ds(24, 27, stride=PACK), :]
    lane = lax.broadcasted_iota(jnp.int32, misc.shape, 1)
    place = lax.broadcasted_iota(jnp.int32, misc.shape, 0) * 2 + lane
    labels = pltpu.roll(misc, 126, 1)
    mine = (lane < 2) & (misc == myself.astype(jnp.float32))
    none = 1e9
    keys = jnp.where(mine, labels * 64.0 + place.astype(jnp.float32), none)
    first_key = jnp.min(keys)
    first = first_key.astype(jnp.int32)
    second = jnp.min(jnp.where(keys > first_key, keys, none)).astype(jnp.int32)
    lower = (first >> 6 < myself * 8).astype(jnp.int32) + (second >> 6 < myself * 8).astype(
        jnp.int32
    )
    spots = (jnp.where(lower >= 1, 0, 6), jnp.where(lower == 2, 1, 7))
    sources = (ref_ref, dis_ref, vel_ref, acc_ref)
    slot = lower
    for k in range(8):
        stays = owner_ref[k] == myself
        target = jnp.where(stays, slot, spots[0])
        slot = slot + stays.astype(jnp.int32)
        for row in range(COMPS):
            out_ref[pl.ds(row * 8 + target, 1), :] = sources[row // 3][row % 3, k : k + 1, :]
    for key, spot in zip((first, second), spots):
        base = ((key & 63) >> 1) * PACK + (key & 1) * COMPS
        for row in range(COMPS):
            out_ref[pl.ds(row * 8 + spot, 1), :] = cand_ref[pl.ds(base + row, 1), :]
    out_ref[96:104, :] = jnp.broadcast_to(jnp.max(tops_ref[...], axis=0, keepdims=True), (8, 128))


def force_kernel(
    pair_ref,
    count_ref,
    source_ref,
    rounds_ref,
    around_ref,
    bits_ref,
    keep_ref,
    dis_ref,
    vel_ref,
    acc_ref,
    raw_ref,
    ext_ref,
    left_ref,
    sums0_ref,
    sums1_ref,
    sums2_ref,
    sums3_ref,
):
    pairs = pair_ref.shape[1]
    fastest = around_ref[96:104, :]
    for cell in range(1, 27):
        fastest = jnp.maximum(fastest, around_ref[cell * CELL + 96 : cell * CELL + 104, :])
    timestep = courant / (fastest + 1e-06)
    half_step = 0.5 * timestep

    def own(c):
        start = 13 * CELL + 8 * c
        return around_ref[start : start + 8, :]

    for c in range(3):
        halfway = own(6 + c) + half_step * own(9 + c)
        shifted = own(3 + c) + timestep * halfway
        dis_ref[c] = shifted
        vel_ref[c] = halfway
        ext_ref[c * 32 : c * 32 + 8, :] = own(c)
        ext_ref[(3 + c) * 32 : (3 + c) * 32 + 8, :] = shifted

    for g in range(24):
        start = source_ref[g]
        for c in range(COMPS):
            raw_ref[c * 24 + g : c * 24 + g + 1, :] = around_ref[pl.ds(start + 8 * c, 1), :]

    for c in range(3):
        for t in range(3):

            def raw(n):
                return raw_ref[n * 24 + t * 8 : n * 24 + t * 8 + 8, :]

            halfway = raw(6 + c) + half_step * raw(9 + c)
            row = 8 + t * 8
            ext_ref[c * 32 + row : c * 32 + row + 8, :] = raw(c)
            ext_ref[(3 + c) * 32 + row : (3 + c) * 32 + row + 8, :] = raw(3 + c) + timestep * halfway

    sums_refs = (sums0_ref, sums1_ref, sums2_ref, sums3_ref)
    for k in range(24):
        for sums_ref in sums_refs:
            sums_ref[k] = jnp.zeros((8, 128), jnp.float32)

    count = count_ref[0]
    keep = keep_ref[...]
    row = lax.broadcasted_iota(jnp.int32, (8, 128), 0)
    upper = row < 4
    first = (row & 3) * 32

    def spread(c, one, other):
        return jnp.where(
            upper,
            jnp.broadcast_to(ext_ref[pl.ds(c * 32 + one, 1), :], (8, 128)),
            jnp.broadcast_to(ext_ref[pl.ds(c * 32 + other, 1), :], (8, 128)),
        )

    def take_round(word, here, table, force):
        below = word - 1
        particle = (lax.population_count(below & ~word) + first) & 127
        there = [by_lane(table[c], particle) for c in range(6)]
        gap = [there[c] - here[c] for c in range(3)]
        now = [gap[c] + (there[3 + c] - here[3 + c]) for c in range(3)]
        rest2 = gap[0] * gap[0] + gap[1] * gap[1] + gap[2] * gap[2]
        now2 = now[0] * now[0] + now[1] * now[1] + now[2] * now[2]
        scaled = lax.rsqrt(rest2) - lax.rsqrt(now2)
        scaled = jnp.where(word != 0, scaled, 0.0)
        return word & below, [force[c] + scaled * now[c] for c in range(3)]

    def bonds(p):
        everything = jnp.where(pair_ref[0, p] == pair_ref[1, p], 0, -1)
        live = jnp.where(p < count, -1, 0)
        return bits_ref[pl.ds(p, 8, stride=pairs), :] & (keep | everything) & live

    def advance(u, p, word, rounds):
        home = (pair_ref[0, p], pair_ref[0, p + 1])
        away = (pair_ref[1, p], pair_ref[1, p + 1])
        here = [spread(c, *home) for c in range(6)]
        table = [spread(c, *away) for c in range(6)]
        force = [jnp.zeros((8, 128), jnp.float32) for _ in range(3)]
        for _ in range(rounds):
            word, force = take_round(word, here, table, force)
        left_ref[u] = word
        for c in range(3):
            sums_refs[u][home[0] * 3 + c] += jnp.where(upper, force[c], 0.0)
            sums_refs[u][home[1] * 3 + c] += jnp.where(upper, 0.0, force[c])

    def step(q, carry):
        for u in range(GROUP // 2):
            p = q * GROUP + 2 * u
            advance(u, p, jnp.where(upper, bonds(p), bonds(p + 1)), STEADY)

        def more(r, carry):
            for u in range(GROUP // 2):
                advance(u, q * GROUP + 2 * u, left_ref[u], 1)
            return carry

        lax.fori_loop(STEADY, rounds_ref[q, 0], more, 0)
        return carry

    lax.fori_loop(0, (count + GROUP - 1) // GROUP, step, 0)

    for c in range(3):
        rows = [
            jnp.sum(sum(sums_ref[h * 3 + c] for sums_ref in sums_refs), axis=0, keepdims=True)
            for h in range(8)
        ]
        acceleration = stiffness * jnp.concatenate(rows, axis=0)
        acc_ref[c] = acceleration
        vel_ref[c] = vel_ref[c] + half_step * acceleration


def call_pack(owner, myself, fields, lattice):
    smem = pl.BlockSpec(memory_space=pltpu.SMEM)
    vmem = pl.BlockSpec(memory_space=pltpu.VMEM)
    return pl.pallas_call(
        pack_kernel,
        out_shape=(
            jax.ShapeDtypeStruct((PACK, 128), jnp.float32),
            jax.ShapeDtypeStruct((lattice, 128), jnp.float32),
        ),
        in_specs=[smem, smem] + [vmem] * 4,
        out_specs=(vmem, vmem),
        name="pack",
    )(owner, myself, *fields)


def call_settle(owner, myself, fields, candidates, tops):
    smem = pl.BlockSpec(memory_space=pltpu.SMEM)
    vmem = pl.BlockSpec(memory_space=pltpu.VMEM)
    return pl.pallas_call(
        settle_kernel,
        out_shape=jax.ShapeDtypeStruct((CELL, 128), jnp.float32),
        in_specs=[smem, smem] + [vmem] * 6,
        out_specs=vmem,
        name="settle",
    )(owner, myself, *fields, candidates, tops)


def call_force(pair_blocks, pair_count, sources, around, wide, rounds):
    smem = pl.BlockSpec(memory_space=pltpu.SMEM)
    vmem = pl.BlockSpec(memory_space=pltpu.VMEM)
    keep = jnp.asarray(self_bits())
    tile = jax.ShapeDtypeStruct((3, 8, 128), jnp.float32)
    return pl.pallas_call(
        force_kernel,
        out_shape=(tile, tile, tile),
        in_specs=[smem] * 4 + [vmem] * 3,
        out_specs=(vmem, vmem, vmem),
        scratch_shapes=[
            pltpu.VMEM((COMPS * 24, 128), jnp.float32),
            pltpu.VMEM((6 * 32, 128), jnp.float32),
            pltpu.VMEM((GROUP // 2, 8, 128), jnp.int32),
        ]
        + [pltpu.VMEM((24, 8, 128), jnp.float32)] * 4,
        name="forces",
    )(
        pair_blocks,
        pair_count,
        sources,
        rounds,
        around,
        wide,
        keep,
    )


def shifted_by(shard, axis, amount):
    size = lax.axis_size(axis)
    return lax.ppermute(shard, axis, [(i, (i + amount) % size) for i in range(size)])


def around_index(offset, extent):
    wrapped = offset % extent
    return jnp.where(wrapped == 0, 1, jnp.where(wrapped == 1, 2, 0))


def per_device(
    ref_pos,
    displace,
    velocity,
    acceleration,
    new_owner,
    ghost_ids,
    pair_blocks,
    pair_count,
    bond_bits,
):
    blocks = ref_pos.shape[0]
    size_x, size_y, size_z = (lax.axis_size(axis) for axis in AXES)
    place_x, place_y, place_z = (lax.axis_index(axis) for axis in AXES)
    myself = ((place_x * size_y + place_y) * size_z + place_z).astype(jnp.int32)
    fields = tuple(
        jnp.transpose(field, (1, 0, 2)) for field in (ref_pos, displace, velocity, acceleration)
    )

    lattice = lax.axis_size(LATTICE)
    body, tops = call_pack(new_owner, myself[None], fields, lattice)
    tops = lax.all_to_all(tops, LATTICE, 0, 0, tiled=True)
    for axis in AXES:
        before = shifted_by(body, axis, 1)
        after = shifted_by(body, axis, -1)
        body = jnp.concatenate([before, body, after], axis=0)
    around = call_settle(new_owner, myself[None], fields, body, tops)

    ghost_dev = ghost_ids // blocks
    ghost_slot = ghost_ids % blocks
    sources = (
        around_index(ghost_dev // (size_y * size_z) - place_x, size_x)
        + around_index(ghost_dev // size_z % size_y - place_y, size_y) * 3
        + around_index(ghost_dev % size_z - place_z, size_z) * 9
    ) * CELL + ghost_slot
    sources = sources.astype(jnp.int32)
    for axis in AXES:
        before = shifted_by(around, axis, 1)
        after = shifted_by(around, axis, -1)
        around = jnp.concatenate([before, around, after], axis=0)
    wide, rounds = call_prepare(bond_bits)
    outs = call_force(pair_blocks, pair_count, sources, around, wide, rounds)
    return tuple(jnp.transpose(out, (1, 0, 2)) for out in outs)


def solution(mesh):
    sizes = [mesh.shape[axis] for axis in ("gx", "gy", "gz")]
    split = Mesh(mesh.devices.reshape([n for size in sizes for n in (size // 2, 2)]), ALL)
    wide = P(ALL, None, None)
    in_specs = (wide,) * 4 + (P(ALL), P(ALL), P(None, ALL), P(ALL), wide)

    return jax.shard_map(
        per_device, mesh=split, in_specs=in_specs, out_specs=(wide,) * 3, check_vma=False
    )
```

profile of v0, /device:TPU:1, one launch (start us, length us, event | category | flops | bytes accessed | tf_op | source)
XLA Modules:
  0.0 107.1 jit_solution(7204092817165949977)
XLA Ops:
  0.6 1.5 %pack.1 = (f32[32,128]{1,0:T(8,128)}, f32[64,128]{1,0:T(8,128)}) custom-call(s32[8]{0:T(128)} %owner_ref.3, s32[1]{0:T(128)} %bitcast.1.self_ref, f32[3,8,128]{2,1,0:T(8,128)} %bitcast.17, f32[3,8,128]{2,1,0:T(8,128)} %bitcast.19, f32[3,8,128]{2,1,0:T(8,128)} %bitcast.21, f32[3,8,128]{2,1,0:T(8,128)} %bitcast.23), custom_call_target="tpu_custom_call" | custom-call | tf_op jit(solution)/shard_map/pack/pallas_call | solution.py:291
  2.2 4.8 %collective-permute-start = (f32[32,128]{1,0:T(8,128)}, f32[32,128]{1,0:T(8,128)S(1)}, u32[]{:S(2)}, u32[]{:S(2)}) collective-permute-start(f32[32,128]{1,0:T(8,128)} %get-tuple-element.11), channel_id=1, source_target_pairs={{0,64},{64,128},{128,192},{192,256},{256,320},{320,384},{384,448},... | collective-permute-start | bytes 49160 | tf_op jit(solution)/shard_map/ppermute | solution.py:345
  7.0 8.6 %collective-permute-start.1 = (f32[32,128]{1,0:T(8,128)}, f32[32,128]{1,0:T(8,128)S(1)}, u32[]{:S(2)}, u32[]{:S(2)}) collective-permute-start(f32[32,128]{1,0:T(8,128)} %get-tuple-element.11), channel_id=1, source_target_pairs={{0,448},{64,0},{128,64},{192,128},{256,192},{320,256},{384,320},{4... | collective-permute-start | bytes 49160 | tf_op jit(solution)/shard_map/ppermute | solution.py:345
  15.6 0.0 collective-permute-done
  15.6 0.7 constant_dynamic-update-slice_fusion.1
  16.4 0.3 collective-permute-done.1
  16.7 3.2 %collective-permute-start.2 = (f32[96,128]{1,0:T(8,128)S(1)}, f32[96,128]{1,0:T(8,128)S(1)}, u32[]{:S(2)}, u32[]{:S(2)}) collective-permute-start(f32[96,128]{1,0:T(8,128)S(1)} %constant_dynamic-update-slice_fusion), channel_id=1, source_target_pairs={{0,8},{8,16},{16,24},{24,32},{32,40},{40,48},{48,56},{56,0},{1,9},... | collective-permute-start | bytes 147464 | tf_op jit(solution)/shard_map/ppermute | solution.py:345
  19.9 3.8 %collective-permute-start.3 = (f32[96,128]{1,0:T(8,128)S(1)}, f32[96,128]{1,0:T(8,128)S(1)}, u32[]{:S(2)}, u32[]{:S(2)}) collective-permute-start(f32[96,128]{1,0:T(8,128)S(1)} %constant_dynamic-update-slice_fusion), channel_id=1, source_target_pairs={{0,56},{8,0},{16,8},{24,16},{32,24},{40,32},{48,40},{56,48},{1,57}... | collective-permute-start | bytes 147464 | tf_op jit(solution)/shard_map/ppermute | solution.py:345
  23.7 0.0 collective-permute-done.2
  23.7 0.7 constant_dynamic-update-slice_fusion.5
  24.4 0.5 collective-permute-done.3
  25.0 3.8 %collective-permute-start.4 = (f32[288,128]{1,0:T(8,128)S(1)}, f32[288,128]{1,0:T(8,128)S(1)}, u32[]{:S(2)}, u32[]{:S(2)}) collective-permute-start(f32[288,128]{1,0:T(8,128)S(1)} %constant_dynamic-update-slice_fusion.3), channel_id=1, source_target_pairs={{0,1},{1,2},{2,3},{3,4},{4,5},{5,6},{6,7},{7,0},{8,9},{9,10},{10,1... | collective-permute-start | bytes 442376 | tf_op jit(solution)/shard_map/ppermute | solution.py:345
  28.8 12.5 %all-to-all-start = ((f32[64,1,128]{2,1,0:T(1,128)}), f32[64,1,128]{2,1,0:T(1,128)S(1)}, u32[]{:S(2)}, u32[]{:S(2)}) async-start(f32[64,1,128]{2,1,0:T(1,128)} %bitcast.25), calls=%async_computation | async-start | bytes 65536 | tf_op jit(solution)/shard_map/all_to_all | solution.py:374
  41.3 0.0 collective-permute-start.5
  41.3 0.0 collective-permute-done.4
  41.3 0.7 constant_dynamic-update-slice_fusion.11
  42.1 4.1 %collective-permute-done.5 = f32[288,128]{1,0:T(8,128)S(1)} collective-permute-done((f32[288,128]{1,0:T(8,128)S(1)}, f32[288,128]{1,0:T(8,128)S(1)}, u32[]{:S(2)}, u32[]{:S(2)}) %collective-permute-start.5) | collective-permute-done | bytes 147488 | tf_op jit(solution)/shard_map/ppermute | solution.py:345
  46.2 0.0 copy-start.2
  46.2 8.2 %all-to-all-done = f32[64,1,128]{2,1,0:T(1,128)S(1)} async-done(((f32[64,1,128]{2,1,0:T(1,128)}), f32[64,1,128]{2,1,0:T(1,128)S(1)}, u32[]{:S(2)}, u32[]{:S(2)}) %all-to-all-start) | async-done | bytes 32800 | tf_op jit(solution)/shard_map/all_to_all | solution.py:374
  54.4 0.0 copy-start.3
  54.4 0.0 copy-done.2
  54.4 0.6 copy-done.3
  55.0 2.1 %settle.1 = f32[104,128]{1,0:T(8,128)} custom-call(s32[8]{0:T(128)} %owner_ref.3, s32[1]{0:T(128)} %bitcast.1.self_ref, f32[3,8,128]{2,1,0:T(8,128)} %bitcast.18, f32[3,8,128]{2,1,0:T(8,128)} %bitcast.20, f32[3,8,128]{2,1,0:T(8,128)} %bitcast.22, f32[3,8,128]{2,1,0:T(8,128)} %bitcast.24, f32[864,128]{1,0:T(8,128)} %copy-done.2, f32[64,128]{1,0:T(8,128)} %bitcast.16), custom_call_target="tpu_custom_call" | custom-call | tf_op jit(solution)/shard_map/settle/pallas_call | solution.py:306
  57.1 0.0 copy-start.4
  57.1 3.2 %collective-permute-start.6 = (f32[104,128]{1,0:T(8,128)}, f32[104,128]{1,0:T(8,128)S(1)}, u32[]{:S(2)}, u32[]{:S(2)}) collective-permute-start(f32[104,128]{1,0:T(8,128)} %settle.1), channel_id=1, source_target_pairs={{0,64},{64,128},{128,192},{192,256},{256,320},{320,384},{384,448},... | collective-permute-start | bytes 159752 | tf_op jit(solution)/shard_map/ppermute | solution.py:345
  60.3 3.4 %collective-permute-start.7 = (f32[104,128]{1,0:T(8,128)}, f32[104,128]{1,0:T(8,128)S(1)}, u32[]{:S(2)}, u32[]{:S(2)}) collective-permute-start(f32[104,128]{1,0:T(8,128)} %settle.1), channel_id=1, source_target_pairs={{0,448},{64,0},{128,64},{192,128},{256,192},{320,256},{384,320},{4... | collective-permute-start | bytes 159752 | tf_op jit(solution)/shard_map/ppermute | solution.py:345
  63.7 0.0 collective-permute-done.6
  63.8 1.7 %collective-permute-done.7 = f32[104,128]{1,0:T(8,128)S(1)} collective-permute-done((f32[104,128]{1,0:T(8,128)}, f32[104,128]{1,0:T(8,128)S(1)}, u32[]{:S(2)}, u32[]{:S(2)}) %collective-permute-start.7) | collective-permute-done | bytes 53280 | tf_op jit(solution)/shard_map/ppermute | solution.py:345
  65.4 0.8 pad_maximum_fusion
  66.2 3.1 %collective-permute-start.8 = (f32[312,128]{1,0:T(8,128)S(1)}, f32[312,128]{1,0:T(8,128)S(1)}, u32[]{:S(2)}, u32[]{:S(2)}) collective-permute-start(f32[312,128]{1,0:T(8,128)S(1)} %pad_maximum_fusion), channel_id=1, source_target_pairs={{0,8},{8,16},{16,24},{24,32},{32,40},{40,48},{48,56},{56,0},{1,9},... | collective-permute-start | bytes 479240 | tf_op jit(solution)/shard_map/ppermute | solution.py:345
  69.3 3.4 %collective-permute-start.9 = (f32[312,128]{1,0:T(8,128)S(1)}, f32[312,128]{1,0:T(8,128)S(1)}, u32[]{:S(2)}, u32[]{:S(2)}) collective-permute-start(f32[312,128]{1,0:T(8,128)S(1)} %pad_maximum_fusion), channel_id=1, source_target_pairs={{0,56},{8,0},{16,8},{24,16},{32,24},{40,32},{48,40},{56,48},{1,57}... | collective-permute-start | bytes 479240 | tf_op jit(solution)/shard_map/ppermute | solution.py:345
  72.7 0.7 collective-permute-done.8
  73.5 0.8 constant_dynamic-update-slice_fusion.17
  74.3 1.3 %collective-permute-done.9 = f32[312,128]{1,0:T(8,128)S(1)} collective-permute-done((f32[312,128]{1,0:T(8,128)S(1)}, f32[312,128]{1,0:T(8,128)S(1)}, u32[]{:S(2)}, u32[]{:S(2)}) %collective-permute-start.9) | collective-permute-done | bytes 159776 | tf_op jit(solution)/shard_map/ppermute | solution.py:345
  75.6 0.0 copy-start.1
  75.6 3.4 %collective-permute-start.10 = (f32[936,128]{1,0:T(8,128)S(1)}, f32[936,128]{1,0:T(8,128)S(1)}, u32[]{:S(2)}, u32[]{:S(2)}) collective-permute-start(f32[936,128]{1,0:T(8,128)S(1)} %constant_dynamic-update-slice_fusion.15), channel_id=1, source_target_pairs={{0,1},{1,2},{2,3},{3,4},{4,5},{5,6},{6,7},{7,0},{8,9},{9,10},{10,1... | collective-permute-start | bytes 1437704 | tf_op jit(solution)/shard_map/ppermute | solution.py:345
  79.7 7.6 %prepare.1 = (s32[8,216,128]{2,1,0:T(8,128)}, s32[27,128]{1,0:T(8,128)}) custom-call(s32[12,216,128]{2,1,0:T(8,128)} %bitcast.14), custom_call_target="tpu_custom_call" | custom-call | flops 20000000 | bytes 2200000 | tf_op jit(solution)/shard_map/prepare/pallas_call | solution.py:75
  87.3 0.0 copy-done.4
  87.3 0.6 fusion.source_ref
  87.9 0.0 collective-permute-start.11
  87.9 0.0 collective-permute-done.10
  88.0 0.0 copy-done.1
  88.0 8.0 %collective-permute-done.11 = f32[936,128]{1,0:T(8,128)S(1)} collective-permute-done((f32[936,128]{1,0:T(8,128)S(1)}, f32[936,128]{1,0:T(8,128)S(1)}, u32[]{:S(2)}, u32[]{:S(2)}) %collective-permute-start.11) | collective-permute-done | bytes 479264 | tf_op jit(solution)/shard_map/ppermute | solution.py:345
  96.1 0.0 copy-start
  96.1 1.1 %copy-done = f32[2808,128]{1,0:T(8,128)} copy-done((f32[2808,128]{1,0:T(8,128)}, f32[2808,128]{1,0:T(8,128)S(1)}, u32[]{:S(2)}) %copy-start) | copy-done | bytes 1437720
  97.2 9.9 %forces.1 = (f32[3,8,128]{2,1,0:T(8,128)}, f32[3,8,128]{2,1,0:T(8,128)}, f32[3,8,128]{2,1,0:T(8,128)}) custom-call(s32[2,216]{1,0:T(2,128)} %pair_ref.1, s32[1]{0:T(128)S(6)} %copy.36.count_ref, s32[24]{0:T(128)} %fusion.source_ref, s32[27,128]{1,0:T(8,128)} %get-tuple-element.10.rounds_ref, f32[2808,128]{1,0:T(8,128)} %copy-done, s32[1728,128]{1,0:T(8,128)} %bitcast.15, ...), custom_call_target="tpu_custom_call" | custom-call | tf_op jit(solution)/shard_map/forces/pallas_call | solution.py:320
  (23 shorter events, 0.2 us)
Async XLA Ops:
  2.2 13.4 %collective-permute-start = (f32[32,128]{1,0:T(8,128)}, f32[32,128]{1,0:T(8,128)S(1)}, u32[]{:S(2)}, u32[]{:S(2)}) collective-permute-start(f32[32,128]{1,0:T(8,128)} %get-tuple-element.11), channel_id=1, source_target_pairs={{0,64},{64,128},{128,192},{192,256},{256,320},{320,384},{384,448},... | collective-permute-start | bytes 49160 | tf_op jit(solution)/shard_map/ppermute | solution.py:345
  7.0 9.7 %collective-permute-start.1 = (f32[32,128]{1,0:T(8,128)}, f32[32,128]{1,0:T(8,128)S(1)}, u32[]{:S(2)}, u32[]{:S(2)}) collective-permute-start(f32[32,128]{1,0:T(8,128)} %get-tuple-element.11), channel_id=1, source_target_pairs={{0,448},{64,0},{128,64},{192,128},{256,192},{320,256},{384,320},{4... | collective-permute-start | bytes 49160 | tf_op jit(solution)/shard_map/ppermute | solution.py:345
  16.7 7.0 %collective-permute-start.2 = (f32[96,128]{1,0:T(8,128)S(1)}, f32[96,128]{1,0:T(8,128)S(1)}, u32[]{:S(2)}, u32[]{:S(2)}) collective-permute-start(f32[96,128]{1,0:T(8,128)S(1)} %constant_dynamic-update-slice_fusion), channel_id=1, source_target_pairs={{0,8},{8,16},{16,24},{24,32},{32,40},{40,48},{48,56},{56,0},{1,9},... | collective-permute-start | bytes 147464 | tf_op jit(solution)/shard_map/ppermute | solution.py:345
  19.9 5.1 %collective-permute-start.3 = (f32[96,128]{1,0:T(8,128)S(1)}, f32[96,128]{1,0:T(8,128)S(1)}, u32[]{:S(2)}, u32[]{:S(2)}) collective-permute-start(f32[96,128]{1,0:T(8,128)S(1)} %constant_dynamic-update-slice_fusion), channel_id=1, source_target_pairs={{0,56},{8,0},{16,8},{24,16},{32,24},{40,32},{48,40},{56,48},{1,57}... | collective-permute-start | bytes 147464 | tf_op jit(solution)/shard_map/ppermute | solution.py:345
  25.0 16.3 %collective-permute-start.4 = (f32[288,128]{1,0:T(8,128)S(1)}, f32[288,128]{1,0:T(8,128)S(1)}, u32[]{:S(2)}, u32[]{:S(2)}) collective-permute-start(f32[288,128]{1,0:T(8,128)S(1)} %constant_dynamic-update-slice_fusion.3), channel_id=1, source_target_pairs={{0,1},{1,2},{2,3},{3,4},{4,5},{5,6},{6,7},{7,0},{8,9},{9,10},{10,1... | collective-permute-start | bytes 442376 | tf_op jit(solution)/shard_map/ppermute | solution.py:345
  28.8 25.7 %all-to-all-start = ((f32[64,1,128]{2,1,0:T(1,128)}), f32[64,1,128]{2,1,0:T(1,128)S(1)}, u32[]{:S(2)}, u32[]{:S(2)}) async-start(f32[64,1,128]{2,1,0:T(1,128)} %bitcast.25), calls=%async_computation | async-start | bytes 65536 | tf_op jit(solution)/shard_map/all_to_all | solution.py:374
  41.3 4.9 %collective-permute-start.5 = (f32[288,128]{1,0:T(8,128)S(1)}, f32[288,128]{1,0:T(8,128)S(1)}, u32[]{:S(2)}, u32[]{:S(2)}) collective-permute-start(f32[288,128]{1,0:T(8,128)S(1)} %constant_dynamic-update-slice_fusion.3), channel_id=1, source_target_pairs={{0,7},{1,0},{2,1},{3,2},{4,3},{5,4},{6,5},{7,6},{8,15},{9,8},{10,9... | collective-permute-start | bytes 442376 | tf_op jit(solution)/shard_map/ppermute | solution.py:345
  46.2 8.2 %copy-start.2 = (f32[864,128]{1,0:T(8,128)}, f32[864,128]{1,0:T(8,128)S(1)}, u32[]{:S(2)}) copy-start(f32[864,128]{1,0:T(8,128)S(1)} %constant_dynamic-update-slice_fusion.8.cand_ref) | copy-start | bytes 1327108
  54.4 0.6 copy-start.3
  57.1 30.2 %copy-start.4 = (s32[24]{0:T(128)S(1)}, s32[24]{0:T(128)}, u32[]{:S(2)}) copy-start(s32[24]{0:T(128)} %param.15) | copy-start | bytes 292
  57.1 6.6 %collective-permute-start.6 = (f32[104,128]{1,0:T(8,128)}, f32[104,128]{1,0:T(8,128)S(1)}, u32[]{:S(2)}, u32[]{:S(2)}) collective-permute-start(f32[104,128]{1,0:T(8,128)} %settle.1), channel_id=1, source_target_pairs={{0,64},{64,128},{128,192},{192,256},{256,320},{320,384},{384,448},... | collective-permute-start | bytes 159752 | tf_op jit(solution)/shard_map/ppermute | solution.py:345
  60.3 5.1 %collective-permute-start.7 = (f32[104,128]{1,0:T(8,128)}, f32[104,128]{1,0:T(8,128)S(1)}, u32[]{:S(2)}, u32[]{:S(2)}) collective-permute-start(f32[104,128]{1,0:T(8,128)} %settle.1), channel_id=1, source_target_pairs={{0,448},{64,0},{128,64},{192,128},{256,192},{320,256},{384,320},{4... | collective-permute-start | bytes 159752 | tf_op jit(solution)/shard_map/ppermute | solution.py:345
  66.2 7.2 %collective-permute-start.8 = (f32[312,128]{1,0:T(8,128)S(1)}, f32[312,128]{1,0:T(8,128)S(1)}, u32[]{:S(2)}, u32[]{:S(2)}) collective-permute-start(f32[312,128]{1,0:T(8,128)S(1)} %pad_maximum_fusion), channel_id=1, source_target_pairs={{0,8},{8,16},{16,24},{24,32},{32,40},{40,48},{48,56},{56,0},{1,9},... | collective-permute-start | bytes 479240 | tf_op jit(solution)/shard_map/ppermute | solution.py:345
  69.3 6.3 %collective-permute-start.9 = (f32[312,128]{1,0:T(8,128)S(1)}, f32[312,128]{1,0:T(8,128)S(1)}, u32[]{:S(2)}, u32[]{:S(2)}) collective-permute-start(f32[312,128]{1,0:T(8,128)S(1)} %pad_maximum_fusion), channel_id=1, source_target_pairs={{0,56},{8,0},{16,8},{24,16},{32,24},{40,32},{48,40},{56,48},{1,57}... | collective-permute-start | bytes 479240 | tf_op jit(solution)/shard_map/ppermute | solution.py:345
  75.6 12.3 %copy-start.1 = (f32[104,128]{1,0:T(8,128)S(1)}, f32[104,128]{1,0:T(8,128)}, u32[]{:S(2)}) copy-start(f32[104,128]{1,0:T(8,128)} %settle.1) | copy-start | bytes 159748
  75.6 12.3 %collective-permute-start.10 = (f32[936,128]{1,0:T(8,128)S(1)}, f32[936,128]{1,0:T(8,128)S(1)}, u32[]{:S(2)}, u32[]{:S(2)}) collective-permute-start(f32[936,128]{1,0:T(8,128)S(1)} %constant_dynamic-update-slice_fusion.15), channel_id=1, source_target_pairs={{0,1},{1,2},{2,3},{3,4},{4,5},{5,6},{6,7},{7,0},{8,9},{9,10},{10,1... | collective-permute-start | bytes 1437704 | tf_op jit(solution)/shard_map/ppermute | solution.py:345
  87.9 8.1 %collective-permute-start.11 = (f32[936,128]{1,0:T(8,128)S(1)}, f32[936,128]{1,0:T(8,128)S(1)}, u32[]{:S(2)}, u32[]{:S(2)}) collective-permute-start(f32[936,128]{1,0:T(8,128)S(1)} %constant_dynamic-update-slice_fusion.15), channel_id=1, source_target_pairs={{0,7},{1,0},{2,1},{3,2},{4,3},{5,4},{6,5},{7,6},{8,15},{9,8},{10,9... | collective-permute-start | bytes 1437704 | tf_op jit(solution)/shard_map/ppermute | solution.py:345
  96.1 1.1 %copy-start = (f32[2808,128]{1,0:T(8,128)}, f32[2808,128]{1,0:T(8,128)S(1)}, u32[]{:S(2)}) copy-start(f32[2808,128]{1,0:T(8,128)S(1)} %constant_dynamic-update-slice_fusion.20.around_ref) | copy-start | bytes 4313092
where the time goes:
time: 108 us; the launch traced here: 107 us
  starting transfers between devices  53.1 us (49%)
  waiting for transfers between devices  24.8 us (23%)
  Pallas kernels  21.1 us (20%)
  local copies, waits for them, and re-layouts  4.94 us (5%)
  between operations  1.58 us (1%)
  other arithmetic  1.45 us (1%)
    ppermute x12, starting transfers between devices, shifted_by(): lax.ppermute(shard, axis, [(i, (i + amount) % size) for i in range(size)])  40.6 us
    ppermute x12, waiting for transfers between devices, shifted_by(): lax.ppermute(shard, axis, [(i, (i + amount) % size) for i in range(size)])  16.6 us
    all_to_all x1, starting transfers between devices, per_device(): tops = lax.all_to_all(tops, LATTICE, 0, 0, tiled=True)  12.5 us
    pallas_call x1, Pallas kernels, call_force(): pl.pallas_call(force_kernel, out_shape=(tile, tile, tile), in_specs=[smem...  9.93 us
    all_to_all x1, waiting for transfers between devices, per_device(): tops = lax.all_to_all(tops, LATTICE, 0, 0, tiled=True)  8.22 us
    pallas_call x1, Pallas kernels, call_prepare(): pl.pallas_call(prepare_kernel, out_shape=(jax.ShapeDtypeStruct((8, pairs,...  7.6 us
    unnamed x32, local copies, waits for them, and re-layouts  4.87 us
  transfers between devices with their start and end apart: 13, of which 8 were waited for; matrix products, arithmetic and copies ran while one was open for 4% of the time, Pallas kernels for 7%

commit v1 on v0

--- a/solution.py
+++ b/solution.py
@@ -8,12 +8,12 @@
 from jax.sharding import PartitionSpec as P
 
 WORD_BITS = 11
-GX = ("gx_half", "gx_odd")
-GY = ("gy_half", "gy_odd")
-GZ = ("gz_half", "gz_odd")
+GX = ("gx_half", "gx_rest")
+GY = ("gy_half", "gy_rest")
+GZ = ("gz_half", "gz_rest")
 AXES = (GX, GY, GZ)
 ALL = GX + GY + GZ
-LATTICE = ("gx_half", "gy_half", "gz_half")
+HALVES = ("gx_half", "gy_half", "gz_half")
 
 courant = 0.05
 stiffness = 20.0
@@ -63,26 +63,29 @@
             wide_ref[4 + t, pl.ds(start, GROUP), :] = total
             used = lax.population_count(total)
             most = used if most is None else jnp.maximum(most, used)
-        most_ref[pl.ds(g, 1), :] = jnp.full((1, 128), jnp.max(most), jnp.int32)
+        most_ref[pl.ds(g, 1), :] = jnp.max(most, axis=0, keepdims=True)
         return carry
 
-    lax.fori_loop(0, pairs // GROUP, group, 0)
+    lax.fori_loop(0, pairs // GROUP, group, 0, unroll=3)
+    most_ref[...] = jnp.broadcast_to(
+        jnp.max(most_ref[...], axis=1, keepdims=True), most_ref.shape
+    )
 
 
 def call_prepare(bond_bits):
     pairs = bond_bits.shape[0]
-    vmem = pl.BlockSpec(memory_space=pltpu.VMEM)
     wide, most = pl.pallas_call(
         prepare_kernel,
         out_shape=(
-            jax.ShapeDtypeStruct((8, pairs, 128), jnp.int32),
+            pltpu.VMEM((8, pairs, 128), jnp.int32),
             jax.ShapeDtypeStruct((pairs // GROUP, 128), jnp.int32),
         ),
-        in_specs=[vmem],
-        out_specs=(vmem, vmem),
+        in_specs=[VMEM],
+        out_specs=(VMEM, VMEM),
         cost_estimate=pl.CostEstimate(
             flops=20_000_000, bytes_accessed=2_200_000, transcendentals=0
         ),
+        compiler_params=LITTLE,
         name="prepare",
     )(jnp.transpose(bond_bits, (1, 0, 2)))
     return wide.reshape(8 * pairs, 128), most
@@ -94,7 +97,9 @@
     return (~lost).astype(np.uint32).view(np.int32)
 
 
-def pack_kernel(owner_ref, self_ref, ref_ref, dis_ref, vel_ref, acc_ref, out_ref, top_ref):
+def pack_kernel(
+    owner_ref, self_ref, tops_ref, ref_ref, dis_ref, vel_ref, acc_ref, out_ref
+):
     myself = self_ref[0]
     first = jnp.int32(0)
     second = jnp.int32(0)
@@ -118,15 +123,13 @@
     misc = jnp.zeros((8, 128), jnp.float32)
     for place, value in enumerate(values):
         misc = jnp.where(lane == place, value.astype(jnp.float32), misc)
-    speed = jnp.maximum(
-        jnp.maximum(jnp.abs(vel_ref[0]), jnp.abs(vel_ref[1])), jnp.abs(vel_ref[2])
-    )
-    out_ref[24:32, :] = misc
-    top_ref[...] = jnp.full(top_ref.shape, jnp.max(speed), jnp.float32)
+    row = lax.broadcasted_iota(jnp.int32, (8, 128), 0)
+    top = jnp.max(tops_ref[...], axis=0, keepdims=True)
+    out_ref[24:32, :] = jnp.where(row == 0, misc, top)
 
 
 def settle_kernel(
-    owner_ref, self_ref, ref_ref, dis_ref, vel_ref, acc_ref, cand_ref, tops_ref, out_ref
+    owner_ref, self_ref, ref_ref, dis_ref, vel_ref, acc_ref, cand_ref, out_ref
 ):
     myself = self_ref[0]
     misc = cand_ref[pl.ds(24, 27, stride=PACK), :]
@@ -155,7 +158,8 @@
         base = ((key & 63) >> 1) * PACK + (key & 1) * COMPS
         for row in range(COMPS):
             out_ref[pl.ds(row * 8 + spot, 1), :] = cand_ref[pl.ds(base + row, 1), :]
-    out_ref[96:104, :] = jnp.broadcast_to(jnp.max(tops_ref[...], axis=0, keepdims=True), (8, 128))
+    tops = cand_ref[pl.ds(25, 27, stride=PACK), :]
+    out_ref[96:104, :] = jnp.broadcast_to(jnp.max(tops, axis=0, keepdims=True), (8, 128))
 
 
 def force_kernel(
@@ -285,57 +289,62 @@
         vel_ref[c] = vel_ref[c] + half_step * acceleration
 
 
-def call_pack(owner, myself, fields, lattice):
-    smem = pl.BlockSpec(memory_space=pltpu.SMEM)
-    vmem = pl.BlockSpec(memory_space=pltpu.VMEM)
+SMEM = pl.BlockSpec(memory_space=pltpu.SMEM)
+VMEM = pl.BlockSpec(memory_space=pltpu.VMEM)
+
+
+LITTLE = pltpu.CompilerParams(vmem_limit_bytes=8 * 1024 * 1024)
+
+
+def near(value):
+    return pltpu.with_memory_space_constraint(value, pltpu.VMEM)
+
+
+def call_pack(owner, myself, tops, fields):
     return pl.pallas_call(
         pack_kernel,
-        out_shape=(
-            jax.ShapeDtypeStruct((PACK, 128), jnp.float32),
-            jax.ShapeDtypeStruct((lattice, 128), jnp.float32),
-        ),
-        in_specs=[smem, smem] + [vmem] * 4,
-        out_specs=(vmem, vmem),
+        out_shape=pltpu.VMEM((PACK, 128), jnp.float32),
+        in_specs=[SMEM, SMEM] + [VMEM] * 5,
+        out_specs=VMEM,
+        compiler_params=LITTLE,
         name="pack",
-    )(owner, myself, *fields)
-
-
-def call_settle(owner, myself, fields, candidates, tops):
-    smem = pl.BlockSpec(memory_space=pltpu.SMEM)
-    vmem = pl.BlockSpec(memory_space=pltpu.VMEM)
+    )(owner, myself, near(tops), *fields)
+
+
+def call_settle(owner, myself, fields, candidates):
     return pl.pallas_call(
         settle_kernel,
-        out_shape=jax.ShapeDtypeStruct((CELL, 128), jnp.float32),
-        in_specs=[smem, smem] + [vmem] * 6,
-        out_specs=vmem,
+        out_shape=pltpu.VMEM((CELL, 128), jnp.float32),
+        in_specs=[SMEM, SMEM] + [VMEM] * 5,
+        out_specs=VMEM,
+        compiler_params=LITTLE,
         name="settle",
-    )(owner, myself, *fields, candidates, tops)
+    )(owner, myself, *fields, near(candidates))
 
 
 def call_force(pair_blocks, pair_count, sources, around, wide, rounds):
-    smem = pl.BlockSpec(memory_space=pltpu.SMEM)
-    vmem = pl.BlockSpec(memory_space=pltpu.VMEM)
     keep = jnp.asarray(self_bits())
     tile = jax.ShapeDtypeStruct((3, 8, 128), jnp.float32)
     return pl.pallas_call(
         force_kernel,
         out_shape=(tile, tile, tile),
-        in_specs=[smem] * 4 + [vmem] * 3,
-        out_specs=(vmem, vmem, vmem),
+        in_specs=[SMEM] * 4 + [VMEM] * 3,
+        out_specs=(VMEM, VMEM, VMEM),
         scratch_shapes=[
             pltpu.VMEM((COMPS * 24, 128), jnp.float32),
             pltpu.VMEM((6 * 32, 128), jnp.float32),
             pltpu.VMEM((GROUP // 2, 8, 128), jnp.int32),
         ]
         + [pltpu.VMEM((24, 8, 128), jnp.float32)] * 4,
+        compiler_params=LITTLE,
         name="forces",
     )(
         pair_blocks,
         pair_count,
         sources,
         rounds,
-        around,
-        wide,
+        near(around),
+        near(wide),
         keep,
     )
 
@@ -369,14 +378,14 @@
         jnp.transpose(field, (1, 0, 2)) for field in (ref_pos, displace, velocity, acceleration)
     )
 
-    lattice = lax.axis_size(LATTICE)
-    body, tops = call_pack(new_owner, myself[None], fields, lattice)
-    tops = lax.all_to_all(tops, LATTICE, 0, 0, tiled=True)
+    fastest = jnp.max(jnp.abs(velocity))
+    tops = lax.all_to_all(jnp.broadcast_to(fastest, (8, 128)), HALVES, 0, 0, tiled=True)
+    body = call_pack(new_owner, myself[None], tops, fields)
     for axis in AXES:
         before = shifted_by(body, axis, 1)
         after = shifted_by(body, axis, -1)
         body = jnp.concatenate([before, body, after], axis=0)
-    around = call_settle(new_owner, myself[None], fields, body, tops)
+    around = call_settle(new_owner, myself[None], fields, body)
 
     ghost_dev = ghost_ids // blocks
     ghost_slot = ghost_ids % blocks
@@ -397,7 +406,7 @@
 
 def solution(mesh):
     sizes = [mesh.shape[axis] for axis in ("gx", "gy", "gz")]
-    split = Mesh(mesh.devices.reshape([n for size in sizes for n in (size // 2, 2)]), ALL)
+    split = Mesh(mesh.devices.reshape([n for size in sizes for n in (2, size // 2)]), ALL)
     wide = P(ALL, None, None)
     in_specs = (wide,) * 4 + (P(ALL), P(ALL), P(None, ALL), P(ALL), wide)
 

time: 108 us -> 104 us (0.963)
  Pallas kernels: 21.1 us -> 11 us
  waiting for transfers between devices: 24.8 us -> 31.5 us
    pallas_call x4, Pallas kernels: 21.1 us -> 11 us  [the longest x1 9.12 us: call_force(): pl.pallas_call(force_kernel, out_shape=(tile, tile, tile), in_specs=[SMEM...]
    ppermute x12, starting transfers between devices: 40.6 us -> 34.6 us  [shifted_by(): lax.ppermute(shard, axis, [(i, (i + amount) % size) for i in range(size)])]
    all_to_all x1, starting transfers between devices: 12.5 us -> 18.5 us  [per_device(): lax.all_to_all(jnp.broadcast_to(fastest, (8, 128)), HALVES, 0, 0, tiled=T...]
    all_to_all x1, waiting for transfers between devices: 8.22 us -> 13.7 us  [per_device(): lax.all_to_all(jnp.broadcast_to(fastest, (8, 128)), HALVES, 0, 0, tiled=T...]
    reduce_max x0 -> x1, other arithmetic: none -> 1.33 us  [per_device(): fastest = jnp.max(jnp.abs(velocity))]
    broadcast_in_dim x0 -> x1, local copies, waits for them, and re-layouts: none -> 1.24 us  [per_device(): jnp.broadcast_to(fastest, (8, 128))]
    ppermute x12, waiting for transfers between devices: 16.6 us -> 17.8 us  [shifted_by(): lax.ppermute(shard, axis, [(i, (i + amount) % size) for i in range(size)])]
    unnamed x32 -> x48, local copies, waits for them, and re-layouts: 4.87 us -> 3.7 us
  transfers between devices with their start and end apart: 13 -> 13, of which waited for: 8 -> 10; matrix products, arithmetic and copies ran while one was open for 4% -> 0% of each run, Pallas kernels for 7% -> 0%
where the time goes in v1:
time: 104 us
  starting transfers between devices  53.1 us (51%)
  waiting for transfers between devices  31.5 us (30%)
  Pallas kernels  11 us (11%)
  local copies, waits for them, and re-layouts  5 us (5%)
  between operations  1.7 us (2%)
  other arithmetic  1.39 us (1%)
    ppermute x12, starting transfers between devices, shifted_by(): lax.ppermute(shard, axis, [(i, (i + amount) % size) for i in range(size)])  34.6 us
    all_to_all x1, starting transfers between devices, per_device(): lax.all_to_all(jnp.broadcast_to(fastest, (8, 128)), HALVES, 0, 0, tiled=T...  18.5 us
    ppermute x12, waiting for transfers between devices, shifted_by(): lax.ppermute(shard, axis, [(i, (i + amount) % size) for i in range(size)])  17.8 us
    all_to_all x1, waiting for transfers between devices, per_device(): lax.all_to_all(jnp.broadcast_to(fastest, (8, 128)), HALVES, 0, 0, tiled=T...  13.7 us
    pallas_call x1, Pallas kernels, call_force(): pl.pallas_call(force_kernel, out_shape=(tile, tile, tile), in_specs=[SMEM...  9.12 us
    unnamed x48, local copies, waits for them, and re-layouts  3.7 us
  transfers between devices with their start and end apart: 13, of which 10 were waited for; matrix products, arithmetic and copies ran while one was open for 0% of the time, Pallas kernels for 0%

profile of v1, /device:TPU:1, one launch (start us, length us, event | category | flops | bytes accessed | tf_op | source)
XLA Modules:
  0.0 103.7 jit_solution(9792306096944274613)
XLA Ops:
  0.6 0.0 copy-start.2
  0.6 0.0 copy-start.4
  0.7 0.0 copy-start.6
  0.7 0.0 copy-start.8
  0.7 0.0 copy-start.12
  0.7 1.3 %abs_reduce_fusion = f32[]{:T(128)} fusion(f32[8,3,128]{2,0,1:T(8,128)} %param.12), kind=kLoop, calls=%fused_computation.26 | loop fusion | flops 6143 | bytes 12292 | tf_op jit(solution)/shard_map/reduce_max | solution.py:381
  2.0 1.2 %broadcast_in_dim.23 = f32[8,1,128]{2,1,0:T(1,128)} broadcast(f32[]{:T(128)} %abs_reduce_fusion), dimensions={} | broadcast | bytes 4100 | tf_op jit(solution)/shard_map/broadcast_in_dim | solution.py:382
  3.3 18.5 %all-to-all-start = ((f32[8,1,128]{2,1,0:T(1,128)}), f32[8,1,128]{2,1,0:T(1,128)S(1)}, u32[]{:S(2)}, u32[]{:S(2)}) async-start(f32[8,1,128]{2,1,0:T(1,128)} %broadcast_in_dim.23), calls=%async_computation | async-start | bytes 8192 | tf_op jit(solution)/shard_map/all_to_all | solution.py:382
  21.8 13.7 %all-to-all-done = f32[8,1,128]{2,1,0:T(1,128)S(1)} async-done(((f32[8,1,128]{2,1,0:T(1,128)}), f32[8,1,128]{2,1,0:T(1,128)S(1)}, u32[]{:S(2)}, u32[]{:S(2)}) %all-to-all-start) | async-done | bytes 4128 | tf_op jit(solution)/shard_map/all_to_all | solution.py:382
  35.5 0.7 copy-done.1
  36.2 0.7 copy-done.3
  36.9 0.7 copy-done.5
  37.6 0.7 copy-done.7
  38.3 0.7 copy-done.11
  39.0 0.6 pack.1
  39.6 3.1 %collective-permute-start = (f32[32,128]{1,0:T(8,128)S(1)}, f32[32,128]{1,0:T(8,128)S(1)}, u32[]{:S(2)}, u32[]{:S(2)}) collective-permute-start(f32[32,128]{1,0:T(8,128)S(1)} %pack.1), channel_id=1, source_target_pairs={{0,64},{64,128},{128,192},{192,256},{256,320},{320,384},{384,448},... | collective-permute-start | bytes 49160 | tf_op jit(solution)/shard_map/ppermute | solution.py:354
  42.7 3.4 %collective-permute-start.1 = (f32[32,128]{1,0:T(8,128)S(1)}, f32[32,128]{1,0:T(8,128)S(1)}, u32[]{:S(2)}, u32[]{:S(2)}) collective-permute-start(f32[32,128]{1,0:T(8,128)S(1)} %pack.1), channel_id=1, source_target_pairs={{0,448},{64,0},{128,64},{192,128},{256,192},{320,256},{384,320},{4... | collective-permute-start | bytes 49160 | tf_op jit(solution)/shard_map/ppermute | solution.py:354
  46.1 0.0 collective-permute-done
  46.1 1.1 %collective-permute-done.1 = f32[32,128]{1,0:T(8,128)S(1)} collective-permute-done((f32[32,128]{1,0:T(8,128)S(1)}, f32[32,128]{1,0:T(8,128)S(1)}, u32[]{:S(2)}, u32[]{:S(2)}) %collective-permute-start.1) | collective-permute-done | bytes 16416 | tf_op jit(solution)/shard_map/ppermute | solution.py:354
  47.2 2.3 %collective-permute-start.2 = (f32[96,128]{1,0:T(8,128)S(1)}, f32[96,128]{1,0:T(8,128)S(1)}, u32[]{:S(2)}, u32[]{:S(2)}) collective-permute-start(f32[96,128]{1,0:T(8,128)S(1)} %pad_maximum_fusion.1), channel_id=1, source_target_pairs={{0,8},{8,16},{16,24},{24,32},{32,40},{40,48},{48,56},{56,0},{1,9},... | collective-permute-start | bytes 147464 | tf_op jit(solution)/shard_map/ppermute | solution.py:354
  49.5 4.2 %collective-permute-start.3 = (f32[96,128]{1,0:T(8,128)S(1)}, f32[96,128]{1,0:T(8,128)S(1)}, u32[]{:S(2)}, u32[]{:S(2)}) collective-permute-start(f32[96,128]{1,0:T(8,128)S(1)} %pad_maximum_fusion.1), channel_id=1, source_target_pairs={{0,56},{8,0},{16,8},{24,16},{32,24},{40,32},{48,40},{56,48},{1,57}... | collective-permute-start | bytes 147464 | tf_op jit(solution)/shard_map/ppermute | solution.py:354
  53.7 0.0 collective-permute-done.2
  53.7 0.0 copy-start
  53.7 1.1 %collective-permute-done.3 = f32[96,128]{1,0:T(8,128)S(1)} collective-permute-done((f32[96,128]{1,0:T(8,128)S(1)}, f32[96,128]{1,0:T(8,128)S(1)}, u32[]{:S(2)}, u32[]{:S(2)}) %collective-permute-start.3) | collective-permute-done | bytes 49184 | tf_op jit(solution)/shard_map/ppermute | solution.py:354
  54.8 4.9 %collective-permute-start.4 = (f32[288,128]{1,0:T(8,128)S(1)}, f32[288,128]{1,0:T(8,128)S(1)}, u32[]{:S(2)}, u32[]{:S(2)}) collective-permute-start(f32[288,128]{1,0:T(8,128)S(1)} %constant_dynamic-update-slice_fusion), channel_id=1, source_target_pairs={{0,1},{1,2},{2,3},{3,4},{4,5},{5,6},{6,7},{7,0},{8,9},{9,10},{10,1... | collective-permute-start | bytes 442376 | tf_op jit(solution)/shard_map/ppermute | solution.py:354
  59.7 0.0 collective-permute-start.5
  59.7 2.1 %collective-permute-done.4 = f32[288,128]{1,0:T(8,128)S(1)} collective-permute-done((f32[288,128]{1,0:T(8,128)S(1)}, f32[288,128]{1,0:T(8,128)S(1)}, u32[]{:S(2)}, u32[]{:S(2)}) %collective-permute-start.4) | collective-permute-done | bytes 147488 | tf_op jit(solution)/shard_map/ppermute | solution.py:354
  61.9 2.7 %collective-permute-done.5 = f32[288,128]{1,0:T(8,128)S(1)} collective-permute-done((f32[288,128]{1,0:T(8,128)S(1)}, f32[288,128]{1,0:T(8,128)S(1)}, u32[]{:S(2)}, u32[]{:S(2)}) %collective-permute-start.5) | collective-permute-done | bytes 147488 | tf_op jit(solution)/shard_map/ppermute | solution.py:354
  64.6 0.0 copy-done.2
  64.6 0.0 copy-done.4
  64.6 0.9 settle.1
  65.5 0.0 copy-start.13
  65.5 3.1 %collective-permute-start.6 = (f32[104,128]{1,0:T(8,128)S(1)}, f32[104,128]{1,0:T(8,128)S(1)}, u32[]{:S(2)}, u32[]{:S(2)}) collective-permute-start(f32[104,128]{1,0:T(8,128)S(1)} %settle.1), channel_id=1, source_target_pairs={{0,64},{64,128},{128,192},{192,256},{256,320},{320,384},{384,448},... | collective-permute-start | bytes 159752 | tf_op jit(solution)/shard_map/ppermute | solution.py:354
  68.6 3.4 %collective-permute-start.7 = (f32[104,128]{1,0:T(8,128)S(1)}, f32[104,128]{1,0:T(8,128)S(1)}, u32[]{:S(2)}, u32[]{:S(2)}) collective-permute-start(f32[104,128]{1,0:T(8,128)S(1)} %settle.1), channel_id=1, source_target_pairs={{0,448},{64,0},{128,64},{192,128},{256,192},{320,256},{384,320},{4... | collective-permute-start | bytes 159752 | tf_op jit(solution)/shard_map/ppermute | solution.py:354
  72.1 0.0 collective-permute-done.6
  72.1 1.4 %collective-permute-done.7 = f32[104,128]{1,0:T(8,128)S(1)} collective-permute-done((f32[104,128]{1,0:T(8,128)S(1)}, f32[104,128]{1,0:T(8,128)S(1)}, u32[]{:S(2)}, u32[]{:S(2)}) %collective-permute-start.7) | collective-permute-done | bytes 53280 | tf_op jit(solution)/shard_map/ppermute | solution.py:354
  73.5 2.1 %collective-permute-start.8 = (f32[312,128]{1,0:T(8,128)S(1)}, f32[312,128]{1,0:T(8,128)S(1)}, u32[]{:S(2)}, u32[]{:S(2)}) collective-permute-start(f32[312,128]{1,0:T(8,128)S(1)} %pad_maximum_fusion), channel_id=1, source_target_pairs={{0,8},{8,16},{16,24},{24,32},{32,40},{40,48},{48,56},{56,0},{1,9},... | collective-permute-start | bytes 479240 | tf_op jit(solution)/shard_map/ppermute | solution.py:354
  75.6 5.0 %collective-permute-start.9 = (f32[312,128]{1,0:T(8,128)S(1)}, f32[312,128]{1,0:T(8,128)S(1)}, u32[]{:S(2)}, u32[]{:S(2)}) collective-permute-start(f32[312,128]{1,0:T(8,128)S(1)} %pad_maximum_fusion), channel_id=1, source_target_pairs={{0,56},{8,0},{16,8},{24,16},{32,24},{40,32},{48,40},{56,48},{1,57}... | collective-permute-start | bytes 479240 | tf_op jit(solution)/shard_map/ppermute | solution.py:354
  80.7 0.7 collective-permute-done.8
  81.4 1.4 %collective-permute-done.9 = f32[312,128]{1,0:T(8,128)S(1)} collective-permute-done((f32[312,128]{1,0:T(8,128)S(1)}, f32[312,128]{1,0:T(8,128)S(1)}, u32[]{:S(2)}, u32[]{:S(2)}) %collective-permute-start.9) | collective-permute-done | bytes 159776 | tf_op jit(solution)/shard_map/ppermute | solution.py:354
  82.9 2.1 %collective-permute-start.10 = (f32[936,128]{1,0:T(8,128)S(1)}, f32[936,128]{1,0:T(8,128)S(1)}, u32[]{:S(2)}, u32[]{:S(2)}) collective-permute-start(f32[936,128]{1,0:T(8,128)S(1)} %constant_dynamic-update-slice_fusion.12), channel_id=1, source_target_pairs={{0,1},{1,2},{2,3},{3,4},{4,5},{5,6},{6,7},{7,0},{8,9},{9,10},{10,1... | collective-permute-start | bytes 1437704 | tf_op jit(solution)/shard_map/ppermute | solution.py:354
  85.6 0.4 prepare.1
  86.1 0.0 copy-start.9
  86.1 0.0 copy-start.10
  86.1 1.0 collective-permute-start.11
  87.1 3.5 %collective-permute-done.10 = f32[936,128]{1,0:T(8,128)S(1)} collective-permute-done((f32[936,128]{1,0:T(8,128)S(1)}, f32[936,128]{1,0:T(8,128)S(1)}, u32[]{:S(2)}, u32[]{:S(2)}) %collective-permute-start.10) | collective-permute-done | bytes 479264 | tf_op jit(solution)/shard_map/ppermute | solution.py:354
  90.7 3.8 %collective-permute-done.11 = f32[936,128]{1,0:T(8,128)S(1)} collective-permute-done((f32[936,128]{1,0:T(8,128)S(1)}, f32[936,128]{1,0:T(8,128)S(1)}, u32[]{:S(2)}, u32[]{:S(2)}) %collective-permute-start.11) | collective-permute-done | bytes 479264 | tf_op jit(solution)/shard_map/ppermute | solution.py:354
  94.6 9.1 %forces.1 = (f32[3,8,128]{2,1,0:T(8,128)}, f32[3,8,128]{2,1,0:T(8,128)}, f32[3,8,128]{2,1,0:T(8,128)}) custom-call(s32[2,216]{1,0:T(2,128)S(1)} %copy-done.10, s32[1]{0:T(128)S(6)} %copy.33.count_ref, s32[24]{0:T(128)S(1)} %fusion.source_ref, s32[27,128]{1,0:T(8,128)S(1)} %get-tuple-element.8.rounds_ref, ...), custom_call_target="tpu_custom_call" | custom-call | tf_op jit(solution)/shard_map/forces/pallas_call | solution.py:328
  (39 shorter events, 0.3 us)
Async XLA Ops:
  0.6 63.9 %copy-start.2 = (f32[8,3,128]{2,0,1:T(8,128)S(1)}, f32[8,3,128]{2,0,1:T(8,128)}, u32[]{:S(2)}) copy-start(f32[8,3,128]{2,0,1:T(8,128)} %param.12) | copy-start | bytes 36868
  0.6 63.9 %copy-start.4 = (f32[8,3,128]{2,0,1:T(8,128)S(1)}, f32[8,3,128]{2,0,1:T(8,128)}, u32[]{:S(2)}) copy-start(f32[8,3,128]{2,0,1:T(8,128)} %param.10) | copy-start | bytes 36868
  0.7 63.9 %copy-start.6 = (f32[8,3,128]{2,0,1:T(8,128)S(1)}, f32[8,3,128]{2,0,1:T(8,128)}, u32[]{:S(2)}) copy-start(f32[8,3,128]{2,0,1:T(8,128)} %param.11) | copy-start | bytes 36868
  0.7 63.9 %copy-start.8 = (f32[8,3,128]{2,0,1:T(8,128)S(1)}, f32[8,3,128]{2,0,1:T(8,128)}, u32[]{:S(2)}) copy-start(f32[8,3,128]{2,0,1:T(8,128)} %param.13) | copy-start | bytes 36868
  0.7 63.9 %copy-start.12 = (s32[8]{0:T(128)S(1)}, s32[8]{0:T(128)}, u32[]{:S(2)}) copy-start(s32[8]{0:T(128)} %owner_ref.3) | copy-start | bytes 100
  3.3 32.2 %all-to-all-start = ((f32[8,1,128]{2,1,0:T(1,128)}), f32[8,1,128]{2,1,0:T(1,128)S(1)}, u32[]{:S(2)}, u32[]{:S(2)}) async-start(f32[8,1,128]{2,1,0:T(1,128)} %broadcast_in_dim.23), calls=%async_computation | async-start | bytes 8192 | tf_op jit(solution)/shard_map/all_to_all | solution.py:382
  35.5 0.7 copy-start.1
  36.2 0.7 copy-start.3
  36.9 0.7 copy-start.5
  37.6 0.7 copy-start.7
  38.3 0.7 copy-start.11
  39.6 6.5 %collective-permute-start = (f32[32,128]{1,0:T(8,128)S(1)}, f32[32,128]{1,0:T(8,128)S(1)}, u32[]{:S(2)}, u32[]{:S(2)}) collective-permute-start(f32[32,128]{1,0:T(8,128)S(1)} %pack.1), channel_id=1, source_target_pairs={{0,64},{64,128},{128,192},{192,256},{256,320},{320,384},{384,448},... | collective-permute-start | bytes 49160 | tf_op jit(solution)/shard_map/ppermute | solution.py:354
  42.7 4.5 %collective-permute-start.1 = (f32[32,128]{1,0:T(8,128)S(1)}, f32[32,128]{1,0:T(8,128)S(1)}, u32[]{:S(2)}, u32[]{:S(2)}) collective-permute-start(f32[32,128]{1,0:T(8,128)S(1)} %pack.1), channel_id=1, source_target_pairs={{0,448},{64,0},{128,64},{192,128},{256,192},{320,256},{384,320},{4... | collective-permute-start | bytes 49160 | tf_op jit(solution)/shard_map/ppermute | solution.py:354
  47.2 6.5 %collective-permute-start.2 = (f32[96,128]{1,0:T(8,128)S(1)}, f32[96,128]{1,0:T(8,128)S(1)}, u32[]{:S(2)}, u32[]{:S(2)}) collective-permute-start(f32[96,128]{1,0:T(8,128)S(1)} %pad_maximum_fusion.1), channel_id=1, source_target_pairs={{0,8},{8,16},{16,24},{24,32},{32,40},{40,48},{48,56},{56,0},{1,9},... | collective-permute-start | bytes 147464 | tf_op jit(solution)/shard_map/ppermute | solution.py:354
  49.5 5.4 %collective-permute-start.3 = (f32[96,128]{1,0:T(8,128)S(1)}, f32[96,128]{1,0:T(8,128)S(1)}, u32[]{:S(2)}, u32[]{:S(2)}) collective-permute-start(f32[96,128]{1,0:T(8,128)S(1)} %pad_maximum_fusion.1), channel_id=1, source_target_pairs={{0,56},{8,0},{16,8},{24,16},{32,24},{40,32},{48,40},{56,48},{1,57}... | collective-permute-start | bytes 147464 | tf_op jit(solution)/shard_map/ppermute | solution.py:354
  53.7 31.9 %copy-start = (s32[216,12,128]{2,0,1:T(8,128)S(1)}, s32[216,12,128]{2,0,1:T(8,128)}, u32[]{:S(2)}) copy-start(s32[216,12,128]{2,0,1:T(8,128)} %param.18) | copy-start | bytes 3981316
  54.8 7.0 %collective-permute-start.4 = (f32[288,128]{1,0:T(8,128)S(1)}, f32[288,128]{1,0:T(8,128)S(1)}, u32[]{:S(2)}, u32[]{:S(2)}) collective-permute-start(f32[288,128]{1,0:T(8,128)S(1)} %constant_dynamic-update-slice_fusion), channel_id=1, source_target_pairs={{0,1},{1,2},{2,3},{3,4},{4,5},{5,6},{6,7},{7,0},{8,9},{9,10},{10,1... | collective-permute-start | bytes 442376 | tf_op jit(solution)/shard_map/ppermute | solution.py:354
  59.7 4.9 %collective-permute-start.5 = (f32[288,128]{1,0:T(8,128)S(1)}, f32[288,128]{1,0:T(8,128)S(1)}, u32[]{:S(2)}, u32[]{:S(2)}) collective-permute-start(f32[288,128]{1,0:T(8,128)S(1)} %constant_dynamic-update-slice_fusion), channel_id=1, source_target_pairs={{0,7},{1,0},{2,1},{3,2},{4,3},{5,4},{6,5},{7,6},{8,15},{9,8},{10,9... | collective-permute-start | bytes 442376 | tf_op jit(solution)/shard_map/ppermute | solution.py:354
  65.5 20.5 %copy-start.13 = (s32[24]{0:T(128)S(1)}, s32[24]{0:T(128)}, u32[]{:S(2)}) copy-start(s32[24]{0:T(128)} %param.15) | copy-start | bytes 292
  65.5 6.5 %collective-permute-start.6 = (f32[104,128]{1,0:T(8,128)S(1)}, f32[104,128]{1,0:T(8,128)S(1)}, u32[]{:S(2)}, u32[]{:S(2)}) collective-permute-start(f32[104,128]{1,0:T(8,128)S(1)} %settle.1), channel_id=1, source_target_pairs={{0,64},{64,128},{128,192},{192,256},{256,320},{320,384},{384,448},... | collective-permute-start | bytes 159752 | tf_op jit(solution)/shard_map/ppermute | solution.py:354
  68.6 4.9 %collective-permute-start.7 = (f32[104,128]{1,0:T(8,128)S(1)}, f32[104,128]{1,0:T(8,128)S(1)}, u32[]{:S(2)}, u32[]{:S(2)}) collective-permute-start(f32[104,128]{1,0:T(8,128)S(1)} %settle.1), channel_id=1, source_target_pairs={{0,448},{64,0},{128,64},{192,128},{256,192},{320,256},{384,320},{4... | collective-permute-start | bytes 159752 | tf_op jit(solution)/shard_map/ppermute | solution.py:354
  73.5 7.8 %collective-permute-start.8 = (f32[312,128]{1,0:T(8,128)S(1)}, f32[312,128]{1,0:T(8,128)S(1)}, u32[]{:S(2)}, u32[]{:S(2)}) collective-permute-start(f32[312,128]{1,0:T(8,128)S(1)} %pad_maximum_fusion), channel_id=1, source_target_pairs={{0,8},{8,16},{16,24},{24,32},{32,40},{40,48},{48,56},{56,0},{1,9},... | collective-permute-start | bytes 479240 | tf_op jit(solution)/shard_map/ppermute | solution.py:354
  75.6 7.2 %collective-permute-start.9 = (f32[312,128]{1,0:T(8,128)S(1)}, f32[312,128]{1,0:T(8,128)S(1)}, u32[]{:S(2)}, u32[]{:S(2)}) collective-permute-start(f32[312,128]{1,0:T(8,128)S(1)} %pad_maximum_fusion), channel_id=1, source_target_pairs={{0,56},{8,0},{16,8},{24,16},{32,24},{40,32},{48,40},{56,48},{1,57}... | collective-permute-start | bytes 479240 | tf_op jit(solution)/shard_map/ppermute | solution.py:354
  82.9 7.7 %collective-permute-start.10 = (f32[936,128]{1,0:T(8,128)S(1)}, f32[936,128]{1,0:T(8,128)S(1)}, u32[]{:S(2)}, u32[]{:S(2)}) collective-permute-start(f32[936,128]{1,0:T(8,128)S(1)} %constant_dynamic-update-slice_fusion.12), channel_id=1, source_target_pairs={{0,1},{1,2},{2,3},{3,4},{4,5},{5,6},{6,7},{7,0},{8,9},{9,10},{10,1... | collective-permute-start | bytes 1437704 | tf_op jit(solution)/shard_map/ppermute | solution.py:354
  86.1 8.5 %copy-start.9 = (s32[8,128]{1,0:T(8,128)S(1)}, s32[8,128]{1,0:T(8,128)}, u32[]{:S(2)}) copy-start(s32[8,128]{1,0:T(8,128)} %constant.112.clone.keep_ref) | copy-start | bytes 12292
  86.1 8.5 %copy-start.10 = (s32[2,216]{1,0:T(2,128)S(1)}, s32[2,216]{1,0:T(2,128)}, u32[]{:S(2)}) copy-start(s32[2,216]{1,0:T(2,128)} %pair_ref.1) | copy-start | bytes 5188
  86.1 8.4 %collective-permute-start.11 = (f32[936,128]{1,0:T(8,128)S(1)}, f32[936,128]{1,0:T(8,128)S(1)}, u32[]{:S(2)}, u32[]{:S(2)}) collective-permute-start(f32[936,128]{1,0:T(8,128)S(1)} %constant_dynamic-update-slice_fusion.12), channel_id=1, source_target_pairs={{0,7},{1,0},{2,1},{3,2},{4,3},{5,4},{6,5},{7,6},{8,15},{9,8},{10,9... | collective-permute-start | bytes 1437704 | tf_op jit(solution)/shard_map/ppermute | solution.py:354

commit v2 on v1

--- a/solution.py
+++ b/solution.py
@@ -8,12 +8,12 @@
 from jax.sharding import PartitionSpec as P
 
 WORD_BITS = 11
-GX = ("gx_half", "gx_rest")
-GY = ("gy_half", "gy_rest")
-GZ = ("gz_half", "gz_rest")
+GX = ("gx_half", "gx_odd")
+GY = ("gy_half", "gy_odd")
+GZ = ("gz_half", "gz_odd")
 AXES = (GX, GY, GZ)
 ALL = GX + GY + GZ
-HALVES = ("gx_half", "gy_half", "gz_half")
+LATTICE = ("gx_half", "gy_half", "gz_half")
 
 courant = 0.05
 stiffness = 20.0
@@ -21,7 +21,7 @@
 
 COMPS = 12
 PACK = 32
-CELL = 104
+CELL = 96
 GROUP = 8
 STEADY = 3
 
@@ -97,9 +97,7 @@
     return (~lost).astype(np.uint32).view(np.int32)
 
 
-def pack_kernel(
-    owner_ref, self_ref, tops_ref, ref_ref, dis_ref, vel_ref, acc_ref, out_ref
-):
+def pack_kernel(owner_ref, self_ref, ref_ref, dis_ref, vel_ref, acc_ref, out_ref):
     myself = self_ref[0]
     first = jnp.int32(0)
     second = jnp.int32(0)
@@ -124,12 +122,14 @@
     for place, value in enumerate(values):
         misc = jnp.where(lane == place, value.astype(jnp.float32), misc)
     row = lax.broadcasted_iota(jnp.int32, (8, 128), 0)
-    top = jnp.max(tops_ref[...], axis=0, keepdims=True)
-    out_ref[24:32, :] = jnp.where(row == 0, misc, top)
+    speed = jnp.maximum(
+        jnp.maximum(jnp.abs(vel_ref[0]), jnp.abs(vel_ref[1])), jnp.abs(vel_ref[2])
+    )
+    out_ref[24:32, :] = jnp.where(row == 0, misc, jnp.max(speed))
 
 
 def settle_kernel(
-    owner_ref, self_ref, ref_ref, dis_ref, vel_ref, acc_ref, cand_ref, out_ref
+    owner_ref, self_ref, ref_ref, dis_ref, vel_ref, acc_ref, cand_ref, out_ref, top_ref
 ):
     myself = self_ref[0]
     misc = cand_ref[pl.ds(24, 27, stride=PACK), :]
@@ -159,7 +159,7 @@
         for row in range(COMPS):
             out_ref[pl.ds(row * 8 + spot, 1), :] = cand_ref[pl.ds(base + row, 1), :]
     tops = cand_ref[pl.ds(25, 27, stride=PACK), :]
-    out_ref[96:104, :] = jnp.broadcast_to(jnp.max(tops, axis=0, keepdims=True), (8, 128))
+    top_ref[...] = jnp.broadcast_to(jnp.max(tops, axis=0, keepdims=True), top_ref.shape)
 
 
 def force_kernel(
@@ -168,6 +168,7 @@
     source_ref,
     rounds_ref,
     around_ref,
+    tops_ref,
     bits_ref,
     keep_ref,
     dis_ref,
@@ -182,9 +183,7 @@
     sums3_ref,
 ):
     pairs = pair_ref.shape[1]
-    fastest = around_ref[96:104, :]
-    for cell in range(1, 27):
-        fastest = jnp.maximum(fastest, around_ref[cell * CELL + 96 : cell * CELL + 104, :])
+    fastest = jnp.broadcast_to(jnp.max(tops_ref[...], axis=0, keepdims=True), (8, 128))
     timestep = courant / (fastest + 1e-06)
     half_step = 0.5 * timestep
 
@@ -300,35 +299,42 @@
     return pltpu.with_memory_space_constraint(value, pltpu.VMEM)
 
 
-def call_pack(owner, myself, tops, fields):
+def aside(value):
+    return pltpu.with_memory_space_constraint(value, pltpu.HBM)
+
+
+def call_pack(owner, myself, fields):
     return pl.pallas_call(
         pack_kernel,
         out_shape=pltpu.VMEM((PACK, 128), jnp.float32),
-        in_specs=[SMEM, SMEM] + [VMEM] * 5,
+        in_specs=[SMEM, SMEM] + [VMEM] * 4,
         out_specs=VMEM,
         compiler_params=LITTLE,
         name="pack",
-    )(owner, myself, near(tops), *fields)
-
-
-def call_settle(owner, myself, fields, candidates):
+    )(aside(owner), myself, *(aside(field) for field in fields))
+
+
+def call_settle(owner, myself, fields, candidates, lattice):
     return pl.pallas_call(
         settle_kernel,
-        out_shape=pltpu.VMEM((CELL, 128), jnp.float32),
+        out_shape=(
+            pltpu.VMEM((CELL, 128), jnp.float32),
+            pltpu.VMEM((lattice, 128), jnp.float32),
+        ),
         in_specs=[SMEM, SMEM] + [VMEM] * 5,
-        out_specs=VMEM,
+        out_specs=(VMEM, VMEM),
         compiler_params=LITTLE,
         name="settle",
     )(owner, myself, *fields, near(candidates))
 
 
-def call_force(pair_blocks, pair_count, sources, around, wide, rounds):
+def call_force(pair_blocks, pair_count, sources, around, tops, wide, rounds):
     keep = jnp.asarray(self_bits())
     tile = jax.ShapeDtypeStruct((3, 8, 128), jnp.float32)
     return pl.pallas_call(
         force_kernel,
         out_shape=(tile, tile, tile),
-        in_specs=[SMEM] * 4 + [VMEM] * 3,
+        in_specs=[SMEM] * 4 + [VMEM] * 4,
         out_specs=(VMEM, VMEM, VMEM),
         scratch_shapes=[
             pltpu.VMEM((COMPS * 24, 128), jnp.float32),
@@ -344,6 +350,7 @@
         sources,
         rounds,
         near(around),
+        near(tops),
         near(wide),
         keep,
     )
@@ -378,14 +385,15 @@
         jnp.transpose(field, (1, 0, 2)) for field in (ref_pos, displace, velocity, acceleration)
     )
 
-    fastest = jnp.max(jnp.abs(velocity))
-    tops = lax.all_to_all(jnp.broadcast_to(fastest, (8, 128)), HALVES, 0, 0, tiled=True)
-    body = call_pack(new_owner, myself[None], tops, fields)
+    body = call_pack(new_owner, myself[None], fields)
     for axis in AXES:
         before = shifted_by(body, axis, 1)
         after = shifted_by(body, axis, -1)
         body = jnp.concatenate([before, body, after], axis=0)
-    around = call_settle(new_owner, myself[None], fields, body)
+    around, top = call_settle(
+        new_owner, myself[None], fields, body, lax.axis_size(LATTICE)
+    )
+    tops = lax.all_to_all(top, LATTICE, 0, 0, tiled=True)
 
     ghost_dev = ghost_ids // blocks
     ghost_slot = ghost_ids % blocks
@@ -400,13 +408,13 @@
         after = shifted_by(around, axis, -1)
         around = jnp.concatenate([before, around, after], axis=0)
     wide, rounds = call_prepare(bond_bits)
-    outs = call_force(pair_blocks, pair_count, sources, around, wide, rounds)
+    outs = call_force(pair_blocks, pair_count, sources, around, tops, wide, rounds)
     return tuple(jnp.transpose(out, (1, 0, 2)) for out in outs)
 
 
 def solution(mesh):
     sizes = [mesh.shape[axis] for axis in ("gx", "gy", "gz")]
-    split = Mesh(mesh.devices.reshape([n for size in sizes for n in (2, size // 2)]), ALL)
+    split = Mesh(mesh.devices.reshape([n for size in sizes for n in (size // 2, 2)]), ALL)
     wide = P(ALL, None, None)
     in_specs = (wide,) * 4 + (P(ALL), P(ALL), P(None, ALL), P(ALL), wide)
 

time: 104 us -> 93.9 us (0.903)
  waiting for transfers between devices: 31.5 us -> 24 us
  local copies, waits for them, and re-layouts: 5 us -> 3.42 us
  other arithmetic: 1.39 us -> 0.04 us
    all_to_all x1, waiting for transfers between devices: 13.7 us -> 4.67 us  [per_device(): tops = lax.all_to_all(top, LATTICE, 0, 0, tiled=True)]
    all_to_all x1, starting transfers between devices: 18.5 us -> 11 us  [per_device(): tops = lax.all_to_all(top, LATTICE, 0, 0, tiled=True)]
    ppermute x12, starting transfers between devices: 34.6 us -> 41.7 us  [shifted_by(): lax.ppermute(shard, axis, [(i, (i + amount) % size) for i in range(size)])]
    ppermute x12, waiting for transfers between devices: 17.8 us -> 19.3 us  [shifted_by(): lax.ppermute(shard, axis, [(i, (i + amount) % size) for i in range(size)])]
    reduce_max x1 -> x0, other arithmetic: 1.33 us -> none  [per_device(): fastest = jnp.max(jnp.abs(velocity))]
    broadcast_in_dim x1 -> x0, local copies, waits for them, and re-layouts: 1.24 us -> none  [per_device(): jnp.broadcast_to(fastest, (8, 128))]
    unnamed x48 -> x40, local copies, waits for them, and re-layouts: 3.7 us -> 2.71 us
  transfers between devices with their start and end apart: 13 -> 13, of which waited for: 10 -> 8; matrix products, arithmetic and copies ran while one was open for 0% -> 3% of each run, Pallas kernels for 0% -> 0%
where the time goes in v2:
time: 93.9 us; the launch traced here: 93.5 us
  starting transfers between devices  52.7 us (56%)
  waiting for transfers between devices  24 us (26%)
  Pallas kernels  11.6 us (12%)
  local copies, waits for them, and re-layouts  3.42 us (4%)
  between operations  1.69 us (2%)
    ppermute x12, starting transfers between devices, shifted_by(): lax.ppermute(shard, axis, [(i, (i + amount) % size) for i in range(size)])  41.7 us
    ppermute x12, waiting for transfers between devices, shifted_by(): lax.ppermute(shard, axis, [(i, (i + amount) % size) for i in range(size)])  19.3 us
    all_to_all x1, starting transfers between devices, per_device(): tops = lax.all_to_all(top, LATTICE, 0, 0, tiled=True)  11 us
    pallas_call x1, Pallas kernels, call_force(): pl.pallas_call(force_kernel, out_shape=(tile, tile, tile), in_specs=[SMEM...  9.11 us
    all_to_all x1, waiting for transfers between devices, per_device(): tops = lax.all_to_all(top, LATTICE, 0, 0, tiled=True)  4.67 us
    unnamed x40, local copies, waits for them, and re-layouts  2.71 us
  transfers between devices with their start and end apart: 13, of which 8 were waited for; matrix products, arithmetic and copies ran while one was open for 3% of the time, Pallas kernels for 0%

profile of v2, /device:TPU:1, one launch (start us, length us, event | category | flops | bytes accessed | tf_op | source)
XLA Modules:
  0.0 93.5 jit_solution(6927392259005629442)
XLA Ops:
  0.6 0.0 copy-start.7
  0.6 0.0 copy-start.4
  0.7 0.0 copy-start.3
  0.7 0.0 copy-start.2
  0.7 0.0 copy-start.1
  0.7 0.9 pack.1
  1.6 11.5 %collective-permute-start.1 = (f32[32,128]{1,0:T(8,128)S(1)}, f32[32,128]{1,0:T(8,128)S(1)}, u32[]{:S(2)}, u32[]{:S(2)}) collective-permute-start(f32[32,128]{1,0:T(8,128)S(1)} %pack.1), channel_id=1, source_target_pairs={{0,448},{64,0},{128,64},{192,128},{256,192},{320,256},{384,320},{4... | collective-permute-start | bytes 49160 | tf_op jit(solution)/shard_map/ppermute | solution.py:361
  13.1 1.9 %collective-permute-start = (f32[32,128]{1,0:T(8,128)S(1)}, f32[32,128]{1,0:T(8,128)S(1)}, u32[]{:S(2)}, u32[]{:S(2)}) collective-permute-start(f32[32,128]{1,0:T(8,128)S(1)} %pack.1), channel_id=1, source_target_pairs={{0,64},{64,128},{128,192},{192,256},{256,320},{320,384},{384,448},... | collective-permute-start | bytes 49160 | tf_op jit(solution)/shard_map/ppermute | solution.py:361
  15.1 0.0 collective-permute-done.1
  15.1 3.8 %collective-permute-done = f32[32,128]{1,0:T(8,128)S(1)} collective-permute-done((f32[32,128]{1,0:T(8,128)S(1)}, f32[32,128]{1,0:T(8,128)S(1)}, u32[]{:S(2)}, u32[]{:S(2)}) %collective-permute-start) | collective-permute-done | bytes 16416 | tf_op jit(solution)/shard_map/ppermute | solution.py:361
  18.8 3.2 %collective-permute-start.2 = (f32[96,128]{1,0:T(8,128)S(1)}, f32[96,128]{1,0:T(8,128)S(1)}, u32[]{:S(2)}, u32[]{:S(2)}) collective-permute-start(f32[96,128]{1,0:T(8,128)S(1)} %pad_maximum_fusion), channel_id=1, source_target_pairs={{0,8},{8,16},{16,24},{24,32},{32,40},{40,48},{48,56},{56,0},{1,9},... | collective-permute-start | bytes 147464 | tf_op jit(solution)/shard_map/ppermute | solution.py:361
  22.0 3.8 %collective-permute-start.3 = (f32[96,128]{1,0:T(8,128)S(1)}, f32[96,128]{1,0:T(8,128)S(1)}, u32[]{:S(2)}, u32[]{:S(2)}) collective-permute-start(f32[96,128]{1,0:T(8,128)S(1)} %pad_maximum_fusion), channel_id=1, source_target_pairs={{0,56},{8,0},{16,8},{24,16},{32,24},{40,32},{48,40},{56,48},{1,57}... | collective-permute-start | bytes 147464 | tf_op jit(solution)/shard_map/ppermute | solution.py:361
  25.8 0.0 collective-permute-done.2
  25.9 0.0 copy-start
  25.9 1.1 %collective-permute-done.3 = f32[96,128]{1,0:T(8,128)S(1)} collective-permute-done((f32[96,128]{1,0:T(8,128)S(1)}, f32[96,128]{1,0:T(8,128)S(1)}, u32[]{:S(2)}, u32[]{:S(2)}) %collective-permute-start.3) | collective-permute-done | bytes 49184 | tf_op jit(solution)/shard_map/ppermute | solution.py:361
  27.0 4.5 %collective-permute-start.4 = (f32[288,128]{1,0:T(8,128)S(1)}, f32[288,128]{1,0:T(8,128)S(1)}, u32[]{:S(2)}, u32[]{:S(2)}) collective-permute-start(f32[288,128]{1,0:T(8,128)S(1)} %constant_dynamic-update-slice_fusion), channel_id=1, source_target_pairs={{0,1},{1,2},{2,3},{3,4},{4,5},{5,6},{6,7},{7,0},{8,9},{9,10},{10,1... | collective-permute-start | bytes 442376 | tf_op jit(solution)/shard_map/ppermute | solution.py:361
  31.5 0.0 collective-permute-start.5
  31.5 2.1 %collective-permute-done.4 = f32[288,128]{1,0:T(8,128)S(1)} collective-permute-done((f32[288,128]{1,0:T(8,128)S(1)}, f32[288,128]{1,0:T(8,128)S(1)}, u32[]{:S(2)}, u32[]{:S(2)}) %collective-permute-start.4) | collective-permute-done | bytes 147488 | tf_op jit(solution)/shard_map/ppermute | solution.py:361
  33.7 2.4 %collective-permute-done.5 = f32[288,128]{1,0:T(8,128)S(1)} collective-permute-done((f32[288,128]{1,0:T(8,128)S(1)}, f32[288,128]{1,0:T(8,128)S(1)}, u32[]{:S(2)}, u32[]{:S(2)}) %collective-permute-start.5) | collective-permute-done | bytes 147488 | tf_op jit(solution)/shard_map/ppermute | solution.py:361
  36.1 0.0 copy-done.7
  36.1 0.0 copy-done.4
  36.1 1.2 %settle.1 = (f32[96,128]{1,0:T(8,128)S(1)}, f32[64,128]{1,0:T(8,128)}) custom-call(s32[8]{0:T(128)S(1)} %copy-done.7, s32[1]{0:T(128)} %bitcast.1.self_ref, f32[3,8,128]{2,1,0:T(8,128)S(1)} %bitcast.18, f32[3,8,128]{2,1,0:T(8,128)S(1)} %bitcast.20, f32[3,8,128]{2,1,0:T(8,128)S(1)} %bitcast.22, f32[3,8,128]{2,1,0:T(8,128)S(1)} %bitcast.24, ...), custom_call_target="tpu_custom_call" | custom-call | tf_op jit(solution)/shard_map/settle/pallas_call | solution.py:318
  37.3 2.0 %collective-permute-start.6 = (f32[96,128]{1,0:T(8,128)S(1)}, f32[96,128]{1,0:T(8,128)S(1)}, u32[]{:S(2)}, u32[]{:S(2)}) collective-permute-start(f32[96,128]{1,0:T(8,128)S(1)} %get-tuple-element.11), channel_id=1, source_target_pairs={{0,64},{64,128},{128,192},{192,256},{256,320},{320,384},{384,448},... | collective-permute-start | bytes 147464 | tf_op jit(solution)/shard_map/ppermute | solution.py:361
  39.4 4.6 %collective-permute-start.7 = (f32[96,128]{1,0:T(8,128)S(1)}, f32[96,128]{1,0:T(8,128)S(1)}, u32[]{:S(2)}, u32[]{:S(2)}) collective-permute-start(f32[96,128]{1,0:T(8,128)S(1)} %get-tuple-element.11), channel_id=1, source_target_pairs={{0,448},{64,0},{128,64},{192,128},{256,192},{320,256},{384,320},{4... | collective-permute-start | bytes 147464 | tf_op jit(solution)/shard_map/ppermute | solution.py:361
  43.9 0.0 collective-permute-done.6
  44.0 1.1 %collective-permute-done.7 = f32[96,128]{1,0:T(8,128)S(1)} collective-permute-done((f32[96,128]{1,0:T(8,128)S(1)}, f32[96,128]{1,0:T(8,128)S(1)}, u32[]{:S(2)}, u32[]{:S(2)}) %collective-permute-start.7) | collective-permute-done | bytes 49184 | tf_op jit(solution)/shard_map/ppermute | solution.py:361
  45.1 3.2 %collective-permute-start.8 = (f32[288,128]{1,0:T(8,128)S(1)}, f32[288,128]{1,0:T(8,128)S(1)}, u32[]{:S(2)}, u32[]{:S(2)}) collective-permute-start(f32[288,128]{1,0:T(8,128)S(1)} %constant_dynamic-update-slice_fusion.12), channel_id=1, source_target_pairs={{0,8},{8,16},{16,24},{24,32},{32,40},{40,48},{48,56},{56,0},{1,9},... | collective-permute-start | bytes 442376 | tf_op jit(solution)/shard_map/ppermute | solution.py:361
  48.3 3.5 %collective-permute-start.9 = (f32[288,128]{1,0:T(8,128)S(1)}, f32[288,128]{1,0:T(8,128)S(1)}, u32[]{:S(2)}, u32[]{:S(2)}) collective-permute-start(f32[288,128]{1,0:T(8,128)S(1)} %constant_dynamic-update-slice_fusion.12), channel_id=1, source_target_pairs={{0,56},{8,0},{16,8},{24,16},{32,24},{40,32},{48,40},{56,48},{1,57}... | collective-permute-start | bytes 442376 | tf_op jit(solution)/shard_map/ppermute | solution.py:361
  51.8 0.6 collective-permute-done.8
  52.4 0.7 constant_dynamic-update-slice_fusion.19
  53.0 0.6 constant_dynamic-update-slice_fusion.18
  53.6 0.6 constant_dynamic-update-slice_fusion.17
  54.3 0.6 constant_dynamic-update-slice_fusion.16
  54.9 0.0 collective-permute-done.9
  54.9 0.7 constant_dynamic-update-slice_fusion.15
  55.6 3.5 %collective-permute-start.10 = (f32[864,128]{1,0:T(8,128)}, f32[864,128]{1,0:T(8,128)S(1)}, u32[]{:S(2)}, u32[]{:S(2)}) collective-permute-start(f32[864,128]{1,0:T(8,128)} %constant_dynamic-update-slice_fusion.15), channel_id=1, source_target_pairs={{0,1},{1,2},{2,3},{3,4},{4,5},{5,6},{6,7},{7,0},{8,9},{9,10},{10,1... | collective-permute-start | bytes 1327112 | tf_op jit(solution)/shard_map/ppermute | solution.py:361
  59.7 0.0 copy-done
  59.7 0.4 prepare.1
  60.1 0.0 copy-done.8
  60.1 11.0 %all-to-all-start = ((f32[64,1,128]{2,1,0:T(1,128)}), f32[64,1,128]{2,1,0:T(1,128)S(1)}, u32[]{:S(2)}, u32[]{:S(2)}) async-start(f32[64,1,128]{2,1,0:T(1,128)} %bitcast.7), calls=%async_computation | async-start | bytes 65536 | tf_op jit(solution)/shard_map/all_to_all | solution.py:396
  71.2 0.0 copy-start.5
  71.2 0.0 copy-start.6
  71.2 0.0 collective-permute-start.11
  71.3 0.0 collective-permute-done.10
  71.4 8.3 %collective-permute-done.11 = f32[864,128]{1,0:T(8,128)S(1)} collective-permute-done((f32[864,128]{1,0:T(8,128)}, f32[864,128]{1,0:T(8,128)S(1)}, u32[]{:S(2)}, u32[]{:S(2)}) %collective-permute-start.11) | collective-permute-done | bytes 442400 | tf_op jit(solution)/shard_map/ppermute | solution.py:361
  79.7 4.7 %all-to-all-done = f32[64,1,128]{2,1,0:T(1,128)S(1)} async-done(((f32[64,1,128]{2,1,0:T(1,128)}), f32[64,1,128]{2,1,0:T(1,128)S(1)}, u32[]{:S(2)}, u32[]{:S(2)}) %all-to-all-start) | async-done | bytes 32800 | tf_op jit(solution)/shard_map/all_to_all | solution.py:396
  84.4 0.0 copy-done.6
  84.4 9.1 %forces.1 = (f32[3,8,128]{2,1,0:T(8,128)}, f32[3,8,128]{2,1,0:T(8,128)}, f32[3,8,128]{2,1,0:T(8,128)}) custom-call(s32[2,216]{1,0:T(2,128)S(1)} %copy-done.6, s32[1]{0:T(128)S(6)} %copy.36.count_ref, s32[24]{0:T(128)S(1)} %fusion.source_ref, s32[27,128]{1,0:T(8,128)S(1)} %get-tuple-element.10.rounds_ref, ...), custom_call_target="tpu_custom_call" | custom-call | tf_op jit(solution)/shard_map/forces/pallas_call | solution.py:334
  (29 shorter events, 0.2 us)
Async XLA Ops:
  0.6 35.4 %copy-start.7 = (s32[8]{0:T(128)S(1)}, s32[8]{0:T(128)}, u32[]{:S(2)}) copy-start(s32[8]{0:T(128)} %owner_ref.3) | copy-start | bytes 100
  0.6 35.4 %copy-start.4 = (f32[8,3,128]{2,0,1:T(8,128)S(1)}, f32[8,3,128]{2,0,1:T(8,128)}, u32[]{:S(2)}) copy-start(f32[8,3,128]{2,0,1:T(8,128)} %param.13) | copy-start | bytes 36868
  0.7 35.4 %copy-start.3 = (f32[8,3,128]{2,0,1:T(8,128)S(1)}, f32[8,3,128]{2,0,1:T(8,128)}, u32[]{:S(2)}) copy-start(f32[8,3,128]{2,0,1:T(8,128)} %param.12) | copy-start | bytes 36868
  0.7 35.4 %copy-start.2 = (f32[8,3,128]{2,0,1:T(8,128)S(1)}, f32[8,3,128]{2,0,1:T(8,128)}, u32[]{:S(2)}) copy-start(f32[8,3,128]{2,0,1:T(8,128)} %param.11) | copy-start | bytes 36868
  0.7 35.4 %copy-start.1 = (f32[8,3,128]{2,0,1:T(8,128)S(1)}, f32[8,3,128]{2,0,1:T(8,128)}, u32[]{:S(2)}) copy-start(f32[8,3,128]{2,0,1:T(8,128)} %param.10) | copy-start | bytes 36868
  1.6 13.4 %collective-permute-start.1 = (f32[32,128]{1,0:T(8,128)S(1)}, f32[32,128]{1,0:T(8,128)S(1)}, u32[]{:S(2)}, u32[]{:S(2)}) collective-permute-start(f32[32,128]{1,0:T(8,128)S(1)} %pack.1), channel_id=1, source_target_pairs={{0,448},{64,0},{128,64},{192,128},{256,192},{320,256},{384,320},{4... | collective-permute-start | bytes 49160 | tf_op jit(solution)/shard_map/ppermute | solution.py:361
  13.1 5.7 %collective-permute-start = (f32[32,128]{1,0:T(8,128)S(1)}, f32[32,128]{1,0:T(8,128)S(1)}, u32[]{:S(2)}, u32[]{:S(2)}) collective-permute-start(f32[32,128]{1,0:T(8,128)S(1)} %pack.1), channel_id=1, source_target_pairs={{0,64},{64,128},{128,192},{192,256},{256,320},{320,384},{384,448},... | collective-permute-start | bytes 49160 | tf_op jit(solution)/shard_map/ppermute | solution.py:361
  18.8 7.0 %collective-permute-start.2 = (f32[96,128]{1,0:T(8,128)S(1)}, f32[96,128]{1,0:T(8,128)S(1)}, u32[]{:S(2)}, u32[]{:S(2)}) collective-permute-start(f32[96,128]{1,0:T(8,128)S(1)} %pad_maximum_fusion), channel_id=1, source_target_pairs={{0,8},{8,16},{16,24},{24,32},{32,40},{40,48},{48,56},{56,0},{1,9},... | collective-permute-start | bytes 147464 | tf_op jit(solution)/shard_map/ppermute | solution.py:361
  22.0 5.0 %collective-permute-start.3 = (f32[96,128]{1,0:T(8,128)S(1)}, f32[96,128]{1,0:T(8,128)S(1)}, u32[]{:S(2)}, u32[]{:S(2)}) collective-permute-start(f32[96,128]{1,0:T(8,128)S(1)} %pad_maximum_fusion), channel_id=1, source_target_pairs={{0,56},{8,0},{16,8},{24,16},{32,24},{40,32},{48,40},{56,48},{1,57}... | collective-permute-start | bytes 147464 | tf_op jit(solution)/shard_map/ppermute | solution.py:361
  25.9 33.8 %copy-start = (s32[216,12,128]{2,0,1:T(8,128)S(1)}, s32[216,12,128]{2,0,1:T(8,128)}, u32[]{:S(2)}) copy-start(s32[216,12,128]{2,0,1:T(8,128)} %param.18) | copy-start | bytes 3981316
  27.0 6.6 %collective-permute-start.4 = (f32[288,128]{1,0:T(8,128)S(1)}, f32[288,128]{1,0:T(8,128)S(1)}, u32[]{:S(2)}, u32[]{:S(2)}) collective-permute-start(f32[288,128]{1,0:T(8,128)S(1)} %constant_dynamic-update-slice_fusion), channel_id=1, source_target_pairs={{0,1},{1,2},{2,3},{3,4},{4,5},{5,6},{6,7},{7,0},{8,9},{9,10},{10,1... | collective-permute-start | bytes 442376 | tf_op jit(solution)/shard_map/ppermute | solution.py:361
  31.5 4.6 %collective-permute-start.5 = (f32[288,128]{1,0:T(8,128)S(1)}, f32[288,128]{1,0:T(8,128)S(1)}, u32[]{:S(2)}, u32[]{:S(2)}) collective-permute-start(f32[288,128]{1,0:T(8,128)S(1)} %constant_dynamic-update-slice_fusion), channel_id=1, source_target_pairs={{0,7},{1,0},{2,1},{3,2},{4,3},{5,4},{6,5},{7,6},{8,15},{9,8},{10,9... | collective-permute-start | bytes 442376 | tf_op jit(solution)/shard_map/ppermute | solution.py:361
  37.3 22.8 %copy-start.8 = (s32[24]{0:T(128)S(1)}, s32[24]{0:T(128)}, u32[]{:S(2)}) copy-start(s32[24]{0:T(128)} %param.15) | copy-start | bytes 292
  37.3 6.6 %collective-permute-start.6 = (f32[96,128]{1,0:T(8,128)S(1)}, f32[96,128]{1,0:T(8,128)S(1)}, u32[]{:S(2)}, u32[]{:S(2)}) collective-permute-start(f32[96,128]{1,0:T(8,128)S(1)} %get-tuple-element.11), channel_id=1, source_target_pairs={{0,64},{64,128},{128,192},{192,256},{256,320},{320,384},{384,448},... | collective-permute-start | bytes 147464 | tf_op jit(solution)/shard_map/ppermute | solution.py:361
  39.4 5.7 %collective-permute-start.7 = (f32[96,128]{1,0:T(8,128)S(1)}, f32[96,128]{1,0:T(8,128)S(1)}, u32[]{:S(2)}, u32[]{:S(2)}) collective-permute-start(f32[96,128]{1,0:T(8,128)S(1)} %get-tuple-element.11), channel_id=1, source_target_pairs={{0,448},{64,0},{128,64},{192,128},{256,192},{320,256},{384,320},{4... | collective-permute-start | bytes 147464 | tf_op jit(solution)/shard_map/ppermute | solution.py:361
  45.1 7.3 %collective-permute-start.8 = (f32[288,128]{1,0:T(8,128)S(1)}, f32[288,128]{1,0:T(8,128)S(1)}, u32[]{:S(2)}, u32[]{:S(2)}) collective-permute-start(f32[288,128]{1,0:T(8,128)S(1)} %constant_dynamic-update-slice_fusion.12), channel_id=1, source_target_pairs={{0,8},{8,16},{16,24},{24,32},{32,40},{40,48},{48,56},{56,0},{1,9},... | collective-permute-start | bytes 442376 | tf_op jit(solution)/shard_map/ppermute | solution.py:361
  48.3 6.6 %collective-permute-start.9 = (f32[288,128]{1,0:T(8,128)S(1)}, f32[288,128]{1,0:T(8,128)S(1)}, u32[]{:S(2)}, u32[]{:S(2)}) collective-permute-start(f32[288,128]{1,0:T(8,128)S(1)} %constant_dynamic-update-slice_fusion.12), channel_id=1, source_target_pairs={{0,56},{8,0},{16,8},{24,16},{32,24},{40,32},{48,40},{56,48},{1,57}... | collective-permute-start | bytes 442376 | tf_op jit(solution)/shard_map/ppermute | solution.py:361
  55.6 15.7 %collective-permute-start.10 = (f32[864,128]{1,0:T(8,128)}, f32[864,128]{1,0:T(8,128)S(1)}, u32[]{:S(2)}, u32[]{:S(2)}) collective-permute-start(f32[864,128]{1,0:T(8,128)} %constant_dynamic-update-slice_fusion.15), channel_id=1, source_target_pairs={{0,1},{1,2},{2,3},{3,4},{4,5},{5,6},{6,7},{7,0},{8,9},{9,10},{10,1... | collective-permute-start | bytes 1327112 | tf_op jit(solution)/shard_map/ppermute | solution.py:361
  60.1 24.2 %all-to-all-start = ((f32[64,1,128]{2,1,0:T(1,128)}), f32[64,1,128]{2,1,0:T(1,128)S(1)}, u32[]{:S(2)}, u32[]{:S(2)}) async-start(f32[64,1,128]{2,1,0:T(1,128)} %bitcast.7), calls=%async_computation | async-start | bytes 65536 | tf_op jit(solution)/shard_map/all_to_all | solution.py:396
  71.2 13.2 %copy-start.5 = (s32[8,128]{1,0:T(8,128)S(1)}, s32[8,128]{1,0:T(8,128)}, u32[]{:S(2)}) copy-start(s32[8,128]{1,0:T(8,128)} %constant.107.clone.keep_ref) | copy-start | bytes 12292
  71.2 13.2 %copy-start.6 = (s32[2,216]{1,0:T(2,128)S(1)}, s32[2,216]{1,0:T(2,128)}, u32[]{:S(2)}) copy-start(s32[2,216]{1,0:T(2,128)} %pair_ref.1) | copy-start | bytes 5188
  71.2 8.4 %collective-permute-start.11 = (f32[864,128]{1,0:T(8,128)}, f32[864,128]{1,0:T(8,128)S(1)}, u32[]{:S(2)}, u32[]{:S(2)}) collective-permute-start(f32[864,128]{1,0:T(8,128)} %constant_dynamic-update-slice_fusion.15), channel_id=1, source_target_pairs={{0,7},{1,0},{2,1},{3,2},{4,3},{5,4},{6,5},{7,6},{8,15},{9,8},{10,9... | collective-permute-start | bytes 1327112 | tf_op jit(solution)/shard_map/ppermute | solution.py:361

commit v3 on v2

--- a/solution.py
+++ b/solution.py
@@ -1,3 +1,5 @@
+import functools
+
 import jax
 import jax.numpy as jnp
 import numpy as np
@@ -22,8 +24,10 @@
 COMPS = 12
 PACK = 32
 CELL = 96
-GROUP = 8
-STEADY = 3
+ROWS = 8
+GROUP = 24
+STEADY = 4
+SUMS = 6
 
 
 LANE_GATHER = lax.GatherDimensionNumbers(
@@ -49,8 +53,8 @@
     pairs = words_ref.shape[1]
 
     def group(g, carry):
-        start = pl.multiple_of(g * GROUP, GROUP)
-        words = [words_ref[w, pl.ds(start, GROUP), :] for w in range(12)]
+        start = pl.multiple_of(g * ROWS, ROWS)
+        words = [words_ref[w, pl.ds(start, ROWS), :] for w in range(12)]
         most = None
         for t in range(4):
             total = None
@@ -59,14 +63,14 @@
                 if -WORD_BITS < move < 32:
                     part = words[w] << move if move >= 0 else words[w] >> -move
                     total = part if total is None else total | part
-            wide_ref[t, pl.ds(start, GROUP), :] = total
-            wide_ref[4 + t, pl.ds(start, GROUP), :] = total
+            wide_ref[t, pl.ds(start, ROWS), :] = total
+            wide_ref[4 + t, pl.ds(start, ROWS), :] = total
             used = lax.population_count(total)
             most = used if most is None else jnp.maximum(most, used)
         most_ref[pl.ds(g, 1), :] = jnp.max(most, axis=0, keepdims=True)
         return carry
 
-    lax.fori_loop(0, pairs // GROUP, group, 0, unroll=3)
+    lax.fori_loop(0, pairs // ROWS, group, 0, unroll=3)
     most_ref[...] = jnp.broadcast_to(
         jnp.max(most_ref[...], axis=1, keepdims=True), most_ref.shape
     )
@@ -78,7 +82,7 @@
         prepare_kernel,
         out_shape=(
             pltpu.VMEM((8, pairs, 128), jnp.int32),
-            jax.ShapeDtypeStruct((pairs // GROUP, 128), jnp.int32),
+            jax.ShapeDtypeStruct((pairs // ROWS, 128), jnp.int32),
         ),
         in_specs=[VMEM],
         out_specs=(VMEM, VMEM),
@@ -162,10 +166,35 @@
     top_ref[...] = jnp.broadcast_to(jnp.max(tops, axis=0, keepdims=True), top_ref.shape)
 
 
+def whole(number, divisor):
+    power = divisor.bit_length() - 1
+    return number >> power if divisor == 1 << power else lax.div(number, divisor)
+
+
+def rest(number, divisor):
+    return number & (divisor - 1) if divisor & (divisor - 1) == 0 else lax.rem(number, divisor)
+
+
+def grid_place(device, sizes):
+    return (
+        whole(device, sizes[1] * sizes[2]),
+        rest(whole(device, sizes[2]), sizes[1]),
+        rest(device, sizes[2]),
+    )
+
+
+def around_index(offset, place, extent):
+    wrapped = rest(offset + extent, extent)
+    ahead = (wrapped == 1) == ((place & 1) == 0)
+    return jnp.where(wrapped == 0, 1, jnp.where(ahead, 2, 0))
+
+
 def force_kernel(
+    sizes,
     pair_ref,
     count_ref,
-    source_ref,
+    ghost_ref,
+    self_ref,
     rounds_ref,
     around_ref,
     tops_ref,
@@ -177,10 +206,7 @@
     raw_ref,
     ext_ref,
     left_ref,
-    sums0_ref,
-    sums1_ref,
-    sums2_ref,
-    sums3_ref,
+    *sums_refs,
 ):
     pairs = pair_ref.shape[1]
     fastest = jnp.broadcast_to(jnp.max(tops_ref[...], axis=0, keepdims=True), (8, 128))
@@ -199,8 +225,12 @@
         ext_ref[c * 32 : c * 32 + 8, :] = own(c)
         ext_ref[(3 + c) * 32 : (3 + c) * 32 + 8, :] = shifted
 
+    myself = grid_place(self_ref[0], sizes)
     for g in range(24):
-        start = source_ref[g]
+        block = ghost_ref[g]
+        owner = grid_place(block >> 3, sizes)
+        cells = [around_index(o - m, m, n) for o, m, n in zip(owner, myself, sizes)]
+        start = (cells[0] + 3 * cells[1] + 9 * cells[2]) * CELL + (block & 7)
         for c in range(COMPS):
             raw_ref[c * 24 + g : c * 24 + g + 1, :] = around_ref[pl.ds(start + 8 * c, 1), :]
 
@@ -215,7 +245,6 @@
             ext_ref[c * 32 + row : c * 32 + row + 8, :] = raw(c)
             ext_ref[(3 + c) * 32 + row : (3 + c) * 32 + row + 8, :] = raw(3 + c) + timestep * halfway
 
-    sums_refs = (sums0_ref, sums1_ref, sums2_ref, sums3_ref)
     for k in range(24):
         for sums_ref in sums_refs:
             sums_ref[k] = jnp.zeros((8, 128), jnp.float32)
@@ -260,8 +289,8 @@
             word, force = take_round(word, here, table, force)
         left_ref[u] = word
         for c in range(3):
-            sums_refs[u][home[0] * 3 + c] += jnp.where(upper, force[c], 0.0)
-            sums_refs[u][home[1] * 3 + c] += jnp.where(upper, 0.0, force[c])
+            sums_refs[u % SUMS][home[0] * 3 + c] += jnp.where(upper, force[c], 0.0)
+            sums_refs[u % SUMS][home[1] * 3 + c] += jnp.where(upper, 0.0, force[c])
 
     def step(q, carry):
         for u in range(GROUP // 2):
@@ -273,7 +302,10 @@
                 advance(u, q * GROUP + 2 * u, left_ref[u], 1)
             return carry
 
-        lax.fori_loop(STEADY, rounds_ref[q, 0], more, 0)
+        rounds = rounds_ref[q * (GROUP // ROWS), 0]
+        for n in range(1, GROUP // ROWS):
+            rounds = jnp.maximum(rounds, rounds_ref[q * (GROUP // ROWS) + n, 0])
+        lax.fori_loop(STEADY, rounds, more, 0)
         return carry
 
     lax.fori_loop(0, (count + GROUP - 1) // GROUP, step, 0)
@@ -328,26 +360,27 @@
     )(owner, myself, *fields, near(candidates))
 
 
-def call_force(pair_blocks, pair_count, sources, around, tops, wide, rounds):
+def call_force(sizes, pair_blocks, pair_count, ghost_ids, myself, around, tops, wide, rounds):
     keep = jnp.asarray(self_bits())
     tile = jax.ShapeDtypeStruct((3, 8, 128), jnp.float32)
     return pl.pallas_call(
-        force_kernel,
+        functools.partial(force_kernel, sizes),
         out_shape=(tile, tile, tile),
-        in_specs=[SMEM] * 4 + [VMEM] * 4,
+        in_specs=[SMEM] * 5 + [VMEM] * 4,
         out_specs=(VMEM, VMEM, VMEM),
         scratch_shapes=[
             pltpu.VMEM((COMPS * 24, 128), jnp.float32),
             pltpu.VMEM((6 * 32, 128), jnp.float32),
             pltpu.VMEM((GROUP // 2, 8, 128), jnp.int32),
         ]
-        + [pltpu.VMEM((24, 8, 128), jnp.float32)] * 4,
+        + [pltpu.VMEM((24, 8, 128), jnp.float32)] * SUMS,
         compiler_params=LITTLE,
         name="forces",
     )(
         pair_blocks,
         pair_count,
-        sources,
+        ghost_ids,
+        myself,
         rounds,
         near(around),
         near(tops),
@@ -356,14 +389,11 @@
     )
 
 
-def shifted_by(shard, axis, amount):
+def swapped(shard, axis, odd):
     size = lax.axis_size(axis)
-    return lax.ppermute(shard, axis, [(i, (i + amount) % size) for i in range(size)])
-
-
-def around_index(offset, extent):
-    wrapped = offset % extent
-    return jnp.where(wrapped == 0, 1, jnp.where(wrapped == 1, 2, 0))
+    return lax.ppermute(
+        shard, axis, [(i, (i + 1 if i % 2 == odd else i - 1) % size) for i in range(size)]
+    )
 
 
 def per_device(
@@ -377,38 +407,30 @@
     pair_count,
     bond_bits,
 ):
-    blocks = ref_pos.shape[0]
-    size_x, size_y, size_z = (lax.axis_size(axis) for axis in AXES)
+    sizes = tuple(lax.axis_size(axis) for axis in AXES)
     place_x, place_y, place_z = (lax.axis_index(axis) for axis in AXES)
-    myself = ((place_x * size_y + place_y) * size_z + place_z).astype(jnp.int32)
+    myself = ((place_x * sizes[1] + place_y) * sizes[2] + place_z).astype(jnp.int32)
     fields = tuple(
         jnp.transpose(field, (1, 0, 2)) for field in (ref_pos, displace, velocity, acceleration)
     )
 
     body = call_pack(new_owner, myself[None], fields)
     for axis in AXES:
-        before = shifted_by(body, axis, 1)
-        after = shifted_by(body, axis, -1)
+        before = swapped(body, axis, 1)
+        after = swapped(body, axis, 0)
         body = jnp.concatenate([before, body, after], axis=0)
     around, top = call_settle(
         new_owner, myself[None], fields, body, lax.axis_size(LATTICE)
     )
     tops = lax.all_to_all(top, LATTICE, 0, 0, tiled=True)
 
-    ghost_dev = ghost_ids // blocks
-    ghost_slot = ghost_ids % blocks
-    sources = (
-        around_index(ghost_dev // (size_y * size_z) - place_x, size_x)
-        + around_index(ghost_dev // size_z % size_y - place_y, size_y) * 3
-        + around_index(ghost_dev % size_z - place_z, size_z) * 9
-    ) * CELL + ghost_slot
-    sources = sources.astype(jnp.int32)
     for axis in AXES:
-        before = shifted_by(around, axis, 1)
-        after = shifted_by(around, axis, -1)
+        before = swapped(around, axis, 1)
+        after = swapped(around, axis, 0)
         around = jnp.concatenate([before, around, after], axis=0)
     wide, rounds = call_prepare(bond_bits)
-    outs = call_force(pair_blocks, pair_count, sources, around, tops, wide, rounds)
+    outs = call_force(
+        sizes, pair_blocks, pair_count, ghost_ids, myself[None], around, tops, wide, rounds)
     return tuple(jnp.transpose(out, (1, 0, 2)) for out in outs)
 
 

time: 93.9 us -> 93.3 us (level)
  starting transfers between devices: 52.7 us -> 56.4 us
  Pallas kernels: 11.6 us -> 9.06 us
  waiting for transfers between devices: 24 us -> 22.2 us
    ppermute x12, waiting for transfers between devices: 19.3 us -> 13.2 us  [swapped(): lax.ppermute(shard, axis, [(i, (i + 1 if i % 2 == odd else i - 1) % size)...]
    all_to_all x1, waiting for transfers between devices: 4.67 us -> 9.06 us  [per_device(): tops = lax.all_to_all(top, LATTICE, 0, 0, tiled=True)]
    ppermute x12, starting transfers between devices: 41.7 us -> 45.6 us  [swapped(): lax.ppermute(shard, axis, [(i, (i + 1 if i % 2 == odd else i - 1) % size)...]
    pallas_call x1, Pallas kernels: 9.11 us -> 6.55 us  [call_force(): pl.pallas_call(functools.partial(force_kernel, sizes), out_shape=(tile, t...]
  transfers between devices with their start and end apart: 13 -> 13, of which waited for: 8 -> 9; matrix products, arithmetic and copies ran while one was open for 3% -> 3% of each run, Pallas kernels for 0% -> 0%
where the time goes in v3:
time: 93.3 us; the launch traced here: 92.8 us
  starting transfers between devices  56.4 us (60%)
  waiting for transfers between devices  22.2 us (24%)
  Pallas kernels  9.06 us (10%)
  local copies, waits for them, and re-layouts  3.42 us (4%)
  between operations  1.69 us (2%)
    ppermute x12, starting transfers between devices, swapped(): lax.ppermute(shard, axis, [(i, (i + 1 if i % 2 == odd else i - 1) % size)...  45.6 us
    ppermute x12, waiting for transfers between devices, swapped(): lax.ppermute(shard, axis, [(i, (i + 1 if i % 2 == odd else i - 1) % size)...  13.2 us
    all_to_all x1, starting transfers between devices, per_device(): tops = lax.all_to_all(top, LATTICE, 0, 0, tiled=True)  10.8 us
    all_to_all x1, waiting for transfers between devices, per_device(): tops = lax.all_to_all(top, LATTICE, 0, 0, tiled=True)  9.06 us
    pallas_call x1, Pallas kernels, call_force(): pl.pallas_call(functools.partial(force_kernel, sizes), out_shape=(tile, t...  6.55 us
    unnamed x40, local copies, waits for them, and re-layouts  2.71 us
  transfers between devices with their start and end apart: 13, of which 9 were waited for; matrix products, arithmetic and copies ran while one was open for 3% of the time, Pallas kernels for 0%

profile of v3, /device:TPU:1, one launch (start us, length us, event | category | flops | bytes accessed | tf_op | source)
XLA Modules:
  0.0 92.8 jit_solution(4510231388866405123)
XLA Ops:
  0.6 0.0 copy-start.1
  0.6 0.0 copy-start.2
  0.7 0.0 copy-start.3
  0.7 0.0 copy-start.4
  0.7 0.0 copy-start.6
  0.7 0.9 pack.1
  1.6 11.5 %collective-permute-start = (f32[32,128]{1,0:T(8,128)S(1)}, f32[32,128]{1,0:T(8,128)S(1)}, u32[]{:S(2)}, u32[]{:S(2)}) collective-permute-start(f32[32,128]{1,0:T(8,128)S(1)} %pack.1), channel_id=1, source_target_pairs={{0,448},{64,128},{128,64},{192,256},{256,192},{320,384},{384,320},... | collective-permute-start | bytes 49160 | tf_op jit(solution)/shard_map/ppermute | solution.py:394
  13.1 1.9 %collective-permute-start.1 = (f32[32,128]{1,0:T(8,128)S(1)}, f32[32,128]{1,0:T(8,128)S(1)}, u32[]{:S(2)}, u32[]{:S(2)}) collective-permute-start(f32[32,128]{1,0:T(8,128)S(1)} %pack.1), channel_id=1, source_target_pairs={{0,64},{64,0},{128,192},{192,128},{256,320},{320,256},{384,448},{4... | collective-permute-start | bytes 49160 | tf_op jit(solution)/shard_map/ppermute | solution.py:394
  15.0 0.0 collective-permute-done
  15.1 2.5 %collective-permute-done.1 = f32[32,128]{1,0:T(8,128)S(1)} collective-permute-done((f32[32,128]{1,0:T(8,128)S(1)}, f32[32,128]{1,0:T(8,128)S(1)}, u32[]{:S(2)}, u32[]{:S(2)}) %collective-permute-start.1) | collective-permute-done | bytes 16416 | tf_op jit(solution)/shard_map/ppermute | solution.py:394
  17.6 5.1 %collective-permute-start.2 = (f32[96,128]{1,0:T(8,128)S(1)}, f32[96,128]{1,0:T(8,128)S(1)}, u32[]{:S(2)}, u32[]{:S(2)}) collective-permute-start(f32[96,128]{1,0:T(8,128)S(1)} %pad_maximum_fusion), channel_id=1, source_target_pairs={{0,56},{8,16},{16,8},{24,32},{32,24},{40,48},{48,40},{56,0},{1,57}... | collective-permute-start | bytes 147464 | tf_op jit(solution)/shard_map/ppermute | solution.py:394
  22.7 1.9 %collective-permute-start.3 = (f32[96,128]{1,0:T(8,128)S(1)}, f32[96,128]{1,0:T(8,128)S(1)}, u32[]{:S(2)}, u32[]{:S(2)}) collective-permute-start(f32[96,128]{1,0:T(8,128)S(1)} %pad_maximum_fusion), channel_id=1, source_target_pairs={{0,8},{8,0},{16,24},{24,16},{32,40},{40,32},{48,56},{56,48},{1,9},... | collective-permute-start | bytes 147464 | tf_op jit(solution)/shard_map/ppermute | solution.py:394
  24.6 0.0 collective-permute-done.2
  24.7 0.0 copy-start
  24.7 2.8 %collective-permute-done.3 = f32[96,128]{1,0:T(8,128)S(1)} collective-permute-done((f32[96,128]{1,0:T(8,128)S(1)}, f32[96,128]{1,0:T(8,128)S(1)}, u32[]{:S(2)}, u32[]{:S(2)}) %collective-permute-start.3) | collective-permute-done | bytes 49184 | tf_op jit(solution)/shard_map/ppermute | solution.py:394
  27.5 6.5 %collective-permute-start.4 = (f32[288,128]{1,0:T(8,128)S(1)}, f32[288,128]{1,0:T(8,128)S(1)}, u32[]{:S(2)}, u32[]{:S(2)}) collective-permute-start(f32[288,128]{1,0:T(8,128)S(1)} %constant_dynamic-update-slice_fusion), channel_id=1, source_target_pairs={{0,7},{1,2},{2,1},{3,4},{4,3},{5,6},{6,5},{7,0},{8,15},{9,10},{10,... | collective-permute-start | bytes 442376 | tf_op jit(solution)/shard_map/ppermute | solution.py:394
  34.1 1.9 %collective-permute-start.5 = (f32[288,128]{1,0:T(8,128)S(1)}, f32[288,128]{1,0:T(8,128)S(1)}, u32[]{:S(2)}, u32[]{:S(2)}) collective-permute-start(f32[288,128]{1,0:T(8,128)S(1)} %constant_dynamic-update-slice_fusion), channel_id=1, source_target_pairs={{0,1},{1,0},{2,3},{3,2},{4,5},{5,4},{6,7},{7,6},{8,9},{9,8},{10,11... | collective-permute-start | bytes 442376 | tf_op jit(solution)/shard_map/ppermute | solution.py:394
  36.0 1.2 %collective-permute-done.4 = f32[288,128]{1,0:T(8,128)S(1)} collective-permute-done((f32[288,128]{1,0:T(8,128)S(1)}, f32[288,128]{1,0:T(8,128)S(1)}, u32[]{:S(2)}, u32[]{:S(2)}) %collective-permute-start.4) | collective-permute-done | bytes 147488 | tf_op jit(solution)/shard_map/ppermute | solution.py:394
  37.3 0.1 collective-permute-done.5
  37.4 0.0 copy-done.1
  37.4 0.0 copy-done.2
  37.4 0.0 copy-done.3
  37.4 1.2 %settle.1 = (f32[96,128]{1,0:T(8,128)S(1)}, f32[64,128]{1,0:T(8,128)}) custom-call(s32[8]{0:T(128)S(1)} %copy-done.6, s32[1]{0:T(128)} %bitcast.self_ref, f32[3,8,128]{2,1,0:T(8,128)S(1)} %bitcast.18, f32[3,8,128]{2,1,0:T(8,128)S(1)} %bitcast.20, f32[3,8,128]{2,1,0:T(8,128)S(1)} %bitcast.22, f32[3,8,128]{2,1,0:T(8,128)S(1)} %bitcast.24, ...), custom_call_target="tpu_custom_call" | custom-call | tf_op jit(solution)/shard_map/settle/pallas_call | solution.py:350
  38.6 1.9 %collective-permute-start.6 = (f32[96,128]{1,0:T(8,128)S(1)}, f32[96,128]{1,0:T(8,128)S(1)}, u32[]{:S(2)}, u32[]{:S(2)}) collective-permute-start(f32[96,128]{1,0:T(8,128)S(1)} %get-tuple-element.11), channel_id=1, source_target_pairs={{0,448},{64,128},{128,64},{192,256},{256,192},{320,384},{384,320},... | collective-permute-start | bytes 147464 | tf_op jit(solution)/shard_map/ppermute | solution.py:394
  40.5 1.9 %collective-permute-start.7 = (f32[96,128]{1,0:T(8,128)S(1)}, f32[96,128]{1,0:T(8,128)S(1)}, u32[]{:S(2)}, u32[]{:S(2)}) collective-permute-start(f32[96,128]{1,0:T(8,128)S(1)} %get-tuple-element.11), channel_id=1, source_target_pairs={{0,64},{64,0},{128,192},{192,128},{256,320},{320,256},{384,448},{4... | collective-permute-start | bytes 147464 | tf_op jit(solution)/shard_map/ppermute | solution.py:394
  42.4 2.2 %collective-permute-done.6 = f32[96,128]{1,0:T(8,128)S(1)} collective-permute-done((f32[96,128]{1,0:T(8,128)S(1)}, f32[96,128]{1,0:T(8,128)S(1)}, u32[]{:S(2)}, u32[]{:S(2)}) %collective-permute-start.6) | collective-permute-done | bytes 49184 | tf_op jit(solution)/shard_map/ppermute | solution.py:394
  44.6 0.7 collective-permute-done.7
  45.3 2.3 %collective-permute-start.8 = (f32[288,128]{1,0:T(8,128)S(1)}, f32[288,128]{1,0:T(8,128)S(1)}, u32[]{:S(2)}, u32[]{:S(2)}) collective-permute-start(f32[288,128]{1,0:T(8,128)S(1)} %constant_dynamic-update-slice_fusion.12), channel_id=1, source_target_pairs={{0,56},{8,16},{16,8},{24,32},{32,24},{40,48},{48,40},{56,0},{1,57}... | collective-permute-start | bytes 442376 | tf_op jit(solution)/shard_map/ppermute | solution.py:394
  47.7 3.0 %collective-permute-start.9 = (f32[288,128]{1,0:T(8,128)S(1)}, f32[288,128]{1,0:T(8,128)S(1)}, u32[]{:S(2)}, u32[]{:S(2)}) collective-permute-start(f32[288,128]{1,0:T(8,128)S(1)} %constant_dynamic-update-slice_fusion.12), channel_id=1, source_target_pairs={{0,8},{8,0},{16,24},{24,16},{32,40},{40,32},{48,56},{56,48},{1,9},... | collective-permute-start | bytes 442376 | tf_op jit(solution)/shard_map/ppermute | solution.py:394
  50.6 1.8 %collective-permute-done.8 = f32[288,128]{1,0:T(8,128)S(1)} collective-permute-done((f32[288,128]{1,0:T(8,128)S(1)}, f32[288,128]{1,0:T(8,128)S(1)}, u32[]{:S(2)}, u32[]{:S(2)}) %collective-permute-start.8) | collective-permute-done | bytes 147488 | tf_op jit(solution)/shard_map/ppermute | solution.py:394
  52.4 0.7 constant_dynamic-update-slice_fusion.19
  53.1 0.6 constant_dynamic-update-slice_fusion.18
  53.7 0.6 constant_dynamic-update-slice_fusion.17
  54.3 0.6 constant_dynamic-update-slice_fusion.16
  55.0 0.0 collective-permute-done.9
  55.0 0.7 constant_dynamic-update-slice_fusion.15
  55.6 5.6 %collective-permute-start.10 = (f32[864,128]{1,0:T(8,128)}, f32[864,128]{1,0:T(8,128)S(1)}, u32[]{:S(2)}, u32[]{:S(2)}) collective-permute-start(f32[864,128]{1,0:T(8,128)} %constant_dynamic-update-slice_fusion.15), channel_id=1, source_target_pairs={{0,7},{1,2},{2,1},{3,4},{4,3},{5,6},{6,5},{7,0},{8,15},{9,10},{10,... | collective-permute-start | bytes 1327112 | tf_op jit(solution)/shard_map/ppermute | solution.py:394
  61.9 0.4 prepare.1
  62.3 10.8 %all-to-all-start = ((f32[64,1,128]{2,1,0:T(1,128)}), f32[64,1,128]{2,1,0:T(1,128)S(1)}, u32[]{:S(2)}, u32[]{:S(2)}) async-start(f32[64,1,128]{2,1,0:T(1,128)} %bitcast.7), calls=%async_computation | async-start | bytes 65536 | tf_op jit(solution)/shard_map/all_to_all | solution.py:425
  73.1 0.0 copy-start.5
  73.1 0.0 copy-start.7
  73.1 0.0 copy-start.8
  73.1 2.1 %collective-permute-start.11 = (f32[864,128]{1,0:T(8,128)}, f32[864,128]{1,0:T(8,128)S(1)}, u32[]{:S(2)}, u32[]{:S(2)}) collective-permute-start(f32[864,128]{1,0:T(8,128)} %constant_dynamic-update-slice_fusion.15), channel_id=1, source_target_pairs={{0,1},{1,0},{2,3},{3,2},{4,5},{5,4},{6,7},{7,6},{8,9},{9,8},{10,11... | collective-permute-start | bytes 1327112 | tf_op jit(solution)/shard_map/ppermute | solution.py:394
  75.2 0.0 collective-permute-done.10
  75.3 1.8 %collective-permute-done.11 = f32[864,128]{1,0:T(8,128)S(1)} collective-permute-done((f32[864,128]{1,0:T(8,128)}, f32[864,128]{1,0:T(8,128)S(1)}, u32[]{:S(2)}, u32[]{:S(2)}) %collective-permute-start.11) | collective-permute-done | bytes 442400 | tf_op jit(solution)/shard_map/ppermute | solution.py:394
  77.2 9.1 %all-to-all-done = f32[64,1,128]{2,1,0:T(1,128)S(1)} async-done(((f32[64,1,128]{2,1,0:T(1,128)}), f32[64,1,128]{2,1,0:T(1,128)S(1)}, u32[]{:S(2)}, u32[]{:S(2)}) %all-to-all-start) | async-done | bytes 32800 | tf_op jit(solution)/shard_map/all_to_all | solution.py:425
  86.2 0.0 copy-done.8
  86.2 6.5 %forces.1 = (f32[3,8,128]{2,1,0:T(8,128)}, f32[3,8,128]{2,1,0:T(8,128)}, f32[3,8,128]{2,1,0:T(8,128)}) custom-call(s32[2,216]{1,0:T(2,128)S(1)} %copy-done.7, s32[1]{0:T(128)S(6)} %copy.36.count_ref, s32[24]{0:T(128)S(1)} %copy-done.8, s32[1]{0:T(128)} %bitcast.self_ref, s32[27,128]{1,0:T(8,128)S(1)} %get-tuple-element.10.rounds_ref, ...), custom_call_target="tpu_custom_call" | custom-call | tf_op jit(solution)/shard_map/forces/pallas_call | solution.py:366
  (28 shorter events, 0.2 us)
Async XLA Ops:
  0.6 36.7 %copy-start.1 = (f32[8,3,128]{2,0,1:T(8,128)S(1)}, f32[8,3,128]{2,0,1:T(8,128)}, u32[]{:S(2)}) copy-start(f32[8,3,128]{2,0,1:T(8,128)} %param.10) | copy-start | bytes 36868
  0.6 36.7 %copy-start.2 = (f32[8,3,128]{2,0,1:T(8,128)S(1)}, f32[8,3,128]{2,0,1:T(8,128)}, u32[]{:S(2)}) copy-start(f32[8,3,128]{2,0,1:T(8,128)} %param.11) | copy-start | bytes 36868
  0.7 36.7 %copy-start.3 = (f32[8,3,128]{2,0,1:T(8,128)S(1)}, f32[8,3,128]{2,0,1:T(8,128)}, u32[]{:S(2)}) copy-start(f32[8,3,128]{2,0,1:T(8,128)} %param.12) | copy-start | bytes 36868
  0.7 36.7 %copy-start.4 = (f32[8,3,128]{2,0,1:T(8,128)S(1)}, f32[8,3,128]{2,0,1:T(8,128)}, u32[]{:S(2)}) copy-start(f32[8,3,128]{2,0,1:T(8,128)} %param.13) | copy-start | bytes 36868
  0.7 36.7 %copy-start.6 = (s32[8]{0:T(128)S(1)}, s32[8]{0:T(128)}, u32[]{:S(2)}) copy-start(s32[8]{0:T(128)} %owner_ref.3) | copy-start | bytes 100
  1.6 13.4 %collective-permute-start = (f32[32,128]{1,0:T(8,128)S(1)}, f32[32,128]{1,0:T(8,128)S(1)}, u32[]{:S(2)}, u32[]{:S(2)}) collective-permute-start(f32[32,128]{1,0:T(8,128)S(1)} %pack.1), channel_id=1, source_target_pairs={{0,448},{64,128},{128,64},{192,256},{256,192},{320,384},{384,320},... | collective-permute-start | bytes 49160 | tf_op jit(solution)/shard_map/ppermute | solution.py:394
  13.1 4.5 %collective-permute-start.1 = (f32[32,128]{1,0:T(8,128)S(1)}, f32[32,128]{1,0:T(8,128)S(1)}, u32[]{:S(2)}, u32[]{:S(2)}) collective-permute-start(f32[32,128]{1,0:T(8,128)S(1)} %pack.1), channel_id=1, source_target_pairs={{0,64},{64,0},{128,192},{192,128},{256,320},{320,256},{384,448},{4... | collective-permute-start | bytes 49160 | tf_op jit(solution)/shard_map/ppermute | solution.py:394
  17.6 7.0 %collective-permute-start.2 = (f32[96,128]{1,0:T(8,128)S(1)}, f32[96,128]{1,0:T(8,128)S(1)}, u32[]{:S(2)}, u32[]{:S(2)}) collective-permute-start(f32[96,128]{1,0:T(8,128)S(1)} %pad_maximum_fusion), channel_id=1, source_target_pairs={{0,56},{8,16},{16,8},{24,32},{32,24},{40,48},{48,40},{56,0},{1,57}... | collective-permute-start | bytes 147464 | tf_op jit(solution)/shard_map/ppermute | solution.py:394
  22.7 4.8 %collective-permute-start.3 = (f32[96,128]{1,0:T(8,128)S(1)}, f32[96,128]{1,0:T(8,128)S(1)}, u32[]{:S(2)}, u32[]{:S(2)}) collective-permute-start(f32[96,128]{1,0:T(8,128)S(1)} %pad_maximum_fusion), channel_id=1, source_target_pairs={{0,8},{8,0},{16,24},{24,16},{32,40},{40,32},{48,56},{56,48},{1,9},... | collective-permute-start | bytes 147464 | tf_op jit(solution)/shard_map/ppermute | solution.py:394
  24.7 37.2 %copy-start = (s32[216,12,128]{2,0,1:T(8,128)S(1)}, s32[216,12,128]{2,0,1:T(8,128)}, u32[]{:S(2)}) copy-start(s32[216,12,128]{2,0,1:T(8,128)} %param.18) | copy-start | bytes 3981316
  27.5 9.6 %collective-permute-start.4 = (f32[288,128]{1,0:T(8,128)S(1)}, f32[288,128]{1,0:T(8,128)S(1)}, u32[]{:S(2)}, u32[]{:S(2)}) collective-permute-start(f32[288,128]{1,0:T(8,128)S(1)} %constant_dynamic-update-slice_fusion), channel_id=1, source_target_pairs={{0,7},{1,2},{2,1},{3,4},{4,3},{5,6},{6,5},{7,0},{8,15},{9,10},{10,... | collective-permute-start | bytes 442376 | tf_op jit(solution)/shard_map/ppermute | solution.py:394
  34.1 3.3 %collective-permute-start.5 = (f32[288,128]{1,0:T(8,128)S(1)}, f32[288,128]{1,0:T(8,128)S(1)}, u32[]{:S(2)}, u32[]{:S(2)}) collective-permute-start(f32[288,128]{1,0:T(8,128)S(1)} %constant_dynamic-update-slice_fusion), channel_id=1, source_target_pairs={{0,1},{1,0},{2,3},{3,2},{4,5},{5,4},{6,7},{7,6},{8,9},{9,8},{10,11... | collective-permute-start | bytes 442376 | tf_op jit(solution)/shard_map/ppermute | solution.py:394
  38.6 6.0 %collective-permute-start.6 = (f32[96,128]{1,0:T(8,128)S(1)}, f32[96,128]{1,0:T(8,128)S(1)}, u32[]{:S(2)}, u32[]{:S(2)}) collective-permute-start(f32[96,128]{1,0:T(8,128)S(1)} %get-tuple-element.11), channel_id=1, source_target_pairs={{0,448},{64,128},{128,64},{192,256},{256,192},{320,384},{384,320},... | collective-permute-start | bytes 147464 | tf_op jit(solution)/shard_map/ppermute | solution.py:394
  40.5 4.8 %collective-permute-start.7 = (f32[96,128]{1,0:T(8,128)S(1)}, f32[96,128]{1,0:T(8,128)S(1)}, u32[]{:S(2)}, u32[]{:S(2)}) collective-permute-start(f32[96,128]{1,0:T(8,128)S(1)} %get-tuple-element.11), channel_id=1, source_target_pairs={{0,64},{64,0},{128,192},{192,128},{256,320},{320,256},{384,448},{4... | collective-permute-start | bytes 147464 | tf_op jit(solution)/shard_map/ppermute | solution.py:394
  45.3 7.1 %collective-permute-start.8 = (f32[288,128]{1,0:T(8,128)S(1)}, f32[288,128]{1,0:T(8,128)S(1)}, u32[]{:S(2)}, u32[]{:S(2)}) collective-permute-start(f32[288,128]{1,0:T(8,128)S(1)} %constant_dynamic-update-slice_fusion.12), channel_id=1, source_target_pairs={{0,56},{8,16},{16,8},{24,32},{32,24},{40,48},{48,40},{56,0},{1,57}... | collective-permute-start | bytes 442376 | tf_op jit(solution)/shard_map/ppermute | solution.py:394
  47.7 7.3 %collective-permute-start.9 = (f32[288,128]{1,0:T(8,128)S(1)}, f32[288,128]{1,0:T(8,128)S(1)}, u32[]{:S(2)}, u32[]{:S(2)}) collective-permute-start(f32[288,128]{1,0:T(8,128)S(1)} %constant_dynamic-update-slice_fusion.12), channel_id=1, source_target_pairs={{0,8},{8,0},{16,24},{24,16},{32,40},{40,32},{48,56},{56,48},{1,9},... | collective-permute-start | bytes 442376 | tf_op jit(solution)/shard_map/ppermute | solution.py:394
  55.6 19.5 %collective-permute-start.10 = (f32[864,128]{1,0:T(8,128)}, f32[864,128]{1,0:T(8,128)S(1)}, u32[]{:S(2)}, u32[]{:S(2)}) collective-permute-start(f32[864,128]{1,0:T(8,128)} %constant_dynamic-update-slice_fusion.15), channel_id=1, source_target_pairs={{0,7},{1,2},{2,1},{3,4},{4,3},{5,6},{6,5},{7,0},{8,15},{9,10},{10,... | collective-permute-start | bytes 1327112 | tf_op jit(solution)/shard_map/ppermute | solution.py:394
  62.3 24.0 %all-to-all-start = ((f32[64,1,128]{2,1,0:T(1,128)}), f32[64,1,128]{2,1,0:T(1,128)S(1)}, u32[]{:S(2)}, u32[]{:S(2)}) async-start(f32[64,1,128]{2,1,0:T(1,128)} %bitcast.7), calls=%async_computation | async-start | bytes 65536 | tf_op jit(solution)/shard_map/all_to_all | solution.py:425
  73.1 13.2 %copy-start.5 = (s32[8,128]{1,0:T(8,128)S(1)}, s32[8,128]{1,0:T(8,128)}, u32[]{:S(2)}) copy-start(s32[8,128]{1,0:T(8,128)} %constant.29.clone.keep_ref) | copy-start | bytes 12292
  73.1 13.2 %copy-start.7 = (s32[2,216]{1,0:T(2,128)S(1)}, s32[2,216]{1,0:T(2,128)}, u32[]{:S(2)}) copy-start(s32[2,216]{1,0:T(2,128)} %pair_ref.1) | copy-start | bytes 5188
  73.1 13.1 %copy-start.8 = (s32[24]{0:T(128)S(1)}, s32[24]{0:T(128)}, u32[]{:S(2)}) copy-start(s32[24]{0:T(128)} %ghost_ref.1) | copy-start | bytes 292
  73.1 4.0 %collective-permute-start.11 = (f32[864,128]{1,0:T(8,128)}, f32[864,128]{1,0:T(8,128)S(1)}, u32[]{:S(2)}, u32[]{:S(2)}) collective-permute-start(f32[864,128]{1,0:T(8,128)} %constant_dynamic-update-slice_fusion.15), channel_id=1, source_target_pairs={{0,1},{1,0},{2,3},{3,2},{4,5},{5,4},{6,7},{7,6},{8,9},{9,8},{10,11... | collective-permute-start | bytes 1327112 | tf_op jit(solution)/shard_map/ppermute | solution.py:394
